TPU v7x, 32 devices: a whole 2x2x4 slice. The times are simulated.
32 devices in a mesh: dp: 8 (over z, x), tensor: 4 (over y, core).
Axes of the slice: x: 2, y: 2, z: 4, core: 2. Of those that a mesh axis runs over, the one named last changes fastest.
Arguments:
- hidden_in: bfloat16 [8, 256, 2048], P('dp'), may hold values from -6 to 6
- upstream_grad: bfloat16 [8, 256, 2048], P('dp'), may hold values from -6 to 6
- seq_lengths: int32 [8], replicated, may hold values from 1 to 256, 1536 in all
- position_order: int32 [8], replicated, may hold values from 0 to 7, each once
- query_weight: bfloat16 [2048, 2048], P(None, 'tensor'), may hold values from -0.125 to 0.125
- key_weight: bfloat16 [2048, 2048], P(None, 'tensor'), may hold values from -0.125 to 0.125
- value_weight: bfloat16 [2048, 2048], P(None, 'tensor'), may hold values from -0.125 to 0.125
- output_weight: bfloat16 [2048, 2048], P('tensor'), may hold values from -0.125 to 0.125
- query_gain: float32 [2048], P('tensor'), may hold values from 0.25 to 1.75
- key_gain: float32 [2048], P('tensor'), may hold values from 0.25 to 1.75
- attn_gain: float32 [2048], replicated, may hold values from 0.25 to 1.75
- gate_weight: bfloat16 [2048, 8192], P(None, 'tensor'), may hold values from -0.125 to 0.125
- up_weight: bfloat16 [2048, 8192], P(None, 'tensor'), may hold values from -0.125 to 0.125
- down_weight: bfloat16 [8192, 2048], P('tensor'), may hold values from -0.0625 to 0.0625
- mlp_gain: float32 [2048], replicated, may hold values from 0.25 to 1.75
Outputs:
- layer_out: bfloat16 [8, 256, 2048], P('dp')
- input_grad: bfloat16 [8, 256, 2048], P('dp')
- query_weight_grad: float32 [2048, 2048], P('dp', 'tensor')
- key_weight_grad: float32 [2048, 2048], P('dp', 'tensor')
- value_weight_grad: float32 [2048, 2048], P('dp', 'tensor')
- output_weight_grad: float32 [2048, 2048], P('tensor', 'dp')
- query_gain_grad: float32 [2048], P('tensor')
- key_gain_grad: float32 [2048], P('tensor')
- attn_gain_grad: float32 [2048], replicated
- gate_weight_grad: float32 [2048, 8192], P('dp', 'tensor')
- up_weight_grad: float32 [2048, 8192], P('dp', 'tensor')
- down_weight_grad: float32 [8192, 2048], P('tensor', 'dp')
- mlp_gain_grad: float32 [2048], replicated
- rms_values: float32 [3], replicated
Inputs may be any that keep to these rules, and one draw needn't show every extreme that they name: `seq_lengths`: lengths of the 8 sequences in sequence order; one is exactly 256; they sum to 1536. `position_order`: a permutation: every sequence sits at exactly one data position.
All inputs are finite; a program needn't handle non-finite values.
Results may differ from a plain program's by a relative error of at most 0.019.
Values may be sent and summed in bfloat16 or wider, within the bound.
A program may use at most 192 MiB of HBM per device.

v0:
```python
import functools
import math
import types

import jax
import jax.numpy as jnp
import numpy as np
from jax import lax
from jax.experimental import pallas as pl
from jax.experimental.pallas import tpu as pltpu
from jax.sharding import PartitionSpec as P

D = 2048
HEAD = 128
EPS = 1e-06
F32 = jnp.float32
BF16 = jnp.bfloat16


def matmul(left, right):
    return jnp.dot(left, right, preferred_element_type=F32)


def left_inner(left, right):
    return lax.dot_general(left, right, (((0,), (0,)), ((), ())), preferred_element_type=F32)


def right_inner(left, right):
    return lax.dot_general(left, right, (((1,), (1,)), ((), ())), preferred_element_type=F32)


def rope_tables(rows, width):
    places = jnp.arange(rows, dtype=F32)
    freq = jnp.power(F32(500000.0), -jnp.arange(width // 2, dtype=F32) * (2.0 / width))
    angle = places[:, None] * freq[None, :]
    return (jnp.cos(angle), jnp.sin(angle))


def rope_constants(rows, width):
    half = width // 2
    exponent = -np.arange(half, dtype=np.float32) * np.float32(2.0 / width)
    freq = np.power(np.float32(500000.0), exponent, dtype=np.float32)
    angle = (np.arange(rows, dtype=np.float32)[:, None] * freq[None, :]).astype(np.float64)
    cosine, sine = np.cos(angle), np.sin(angle)
    return (
        jnp.asarray(np.concatenate([cosine, cosine], axis=1), F32),
        jnp.asarray(np.concatenate([-sine, sine], axis=1), F32),
    )


class Grid:
    def __init__(self, count):
        self.count = count
        self.lanes = 2 ** ((count.bit_length() - 1) // 2)
        self.groups = count // self.lanes
        me = lax.axis_index("dp")
        self.group = me // self.lanes
        self.lane = me % self.lanes

    def shift_groups(self, field, step):
        pairs = [
            (g * self.lanes + a, ((g + step) % self.groups) * self.lanes + a)
            for g in range(self.groups)
            for a in range(self.lanes)
        ]
        return lax.ppermute(field, "dp", pairs)

    def shift_lanes(self, field, step):
        pairs = [
            (g * self.lanes + a, g * self.lanes + (a + step) % self.lanes)
            for g in range(self.groups)
            for a in range(self.lanes)
        ]
        return lax.ppermute(field, "dp", pairs)

    def ring(self, field):
        found = []
        for _ in range(self.groups - 1):
            field = self.shift_groups(field, 1)
            found.append(field)
        return found

    def total(self, field):
        step = 1
        while step < self.count:
            field = field + lax.ppermute(
                field, "dp", [(i, i ^ step) for i in range(self.count)]
            )
            step *= 2
        return field


def sibling(field):
    size = lax.axis_size("tensor")
    return lax.ppermute(field, "tensor", [(i, i ^ 1) for i in range(size)])


def across(field):
    size = lax.axis_size("tensor")
    return lax.ppermute(field, "tensor", [(i, (i + 2) % size) for i in range(size)])


def shared_ring(grid, rows_low):
    core = lax.axis_index("tensor") % 2
    half = rows_low.shape[0] // 2
    mine = lax.dynamic_slice_in_dim(rows_low, core * half, half, axis=0)
    pieces = []
    for piece in grid.ring(mine):
        pieces += [piece, sibling(piece)]
    return jnp.concatenate(pieces, axis=0)


SLOTS = 4
TILES = 4
AT = pl.DeviceIdType.MESH
VMEM_CAP = 56 * 2**20


class Team:
    def __init__(self):
        self.row = lax.axis_index("dp")
        self.me = lax.axis_index("tensor")
        self.side = self.me // 2
        self.core = self.me % 2
        self.slot = self.core * 2 + self.side
        self.sibling = self.side * 2 + (1 - self.core)
        self.across = (1 - self.side) * 2 + self.core
        self.far = (1 - self.side) * 2 + (1 - self.core)

    def meet(self, *others):
        barrier = pltpu.get_barrier_semaphore()
        for other in others:
            pl.semaphore_signal(barrier, inc=1, device_id=(self.row, other), device_id_type=AT)
        pl.semaphore_wait(barrier, len(others))

    def copy(self, source, target, send, recv, other):
        return pltpu.make_async_remote_copy(
            src_ref=source,
            dst_ref=target,
            send_sem=send,
            recv_sem=recv,
            device_id=(self.row, other),
            device_id_type=AT,
        )


def at_rows(start, size):
    return pl.ds(pl.multiple_of(start, size), size)


class Reduce:
    def scratch(rows, width):
        shard = rows // SLOTS
        return [
            pltpu.VMEM((rows, width), BF16),
            pltpu.VMEM((3, shard, width), BF16),
            pltpu.VMEM((shard, width), BF16),
            pltpu.VMEM((shard, width), F32),
            pltpu.SemaphoreType.DMA((3, TILES)),
            pltpu.SemaphoreType.DMA((3, TILES)),
        ]

    def __init__(self, team, partial, came, gone, total, send, recv):
        self.team, self.partial, self.came, self.gone, self.total = team, partial, came, gone, total
        self.shard, width = total.shape
        self.tiles = send.shape[1]
        self.tile = width // self.tiles
        self.send, self.recv = send, recv
        self.copies = {}

    def columns(self, tile):
        return pl.ds(tile * self.tile, self.tile)

    def block(self, core, side):
        return at_rows((core * 2 + side) * self.shard, self.shard)

    def launch(self, kind, tile, source, other):
        copy = self.team.copy(
            source,
            self.came.at[kind, :, self.columns(tile)],
            self.send.at[kind, tile],
            self.recv.at[kind, tile],
            other,
        )
        copy.start()
        self.copies[kind, tile] = copy

    def offer(self, tile):
        team, columns = self.team, self.columns(tile)
        for kind, side in ((0, 1 - team.side), (1, team.side)):
            self.launch(
                kind, tile, self.partial.at[self.block(1 - team.core, side), columns], team.sibling
            )

    def pass_on(self, tile):
        team, columns = self.team, self.columns(tile)
        self.copies[0, tile].wait_recv()
        mine = self.partial[self.block(team.core, 1 - team.side), columns].astype(F32)
        self.gone[:, columns] = (mine + self.came[0, :, columns].astype(F32)).astype(BF16)
        self.launch(2, tile, self.gone.at[:, columns], team.across)

    def finish(self, tile):
        team, columns = self.team, self.columns(tile)
        self.copies[1, tile].wait_recv()
        mine = self.partial[self.block(team.core, team.side), columns].astype(F32)
        mine = mine + self.came[1, :, columns].astype(F32)
        self.copies[2, tile].wait_recv()
        self.total[:, columns] = mine + self.came[2, :, columns].astype(F32)

    def settle(self):
        for copy in self.copies.values():
            copy.wait_send()

    def begin(self, make):
        self.copies = {}
        for tile in range(self.tiles):
            make(self.columns(tile))
            self.offer(tile)
            if tile:
                self.pass_on(tile - 1)
        self.pass_on(self.tiles - 1)

    def end(self):
        for tile in range(self.tiles):
            self.finish(tile)
        self.settle()

    def run(self, make):
        self.begin(make)
        self.end()


class Gather:
    scratch = [pltpu.SemaphoreType.DMA((3,)), pltpu.SemaphoreType.DMA((3,))]

    def __init__(self, team, whole, send, recv):
        self.team, self.whole = team, whole
        shard = whole.shape[0] // SLOTS
        mine = whole.at[at_rows(team.slot * shard, shard)]
        theirs = whole.at[at_rows((team.core * 2 + 1 - team.side) * shard, shard)]
        self.across = team.copy(mine, mine, send.at[0], recv.at[0], team.across)
        self.near = team.copy(mine, mine, send.at[1], recv.at[1], team.sibling)
        self.relay = team.copy(theirs, theirs, send.at[2], recv.at[2], team.sibling)

    def start(self):
        self.across.start()
        self.near.start()

    def half(self):
        self.across.wait_recv()
        self.relay.start()

    def finish(self):
        self.across.wait_send()
        self.near.wait()
        self.relay.wait()


class RowSums:
    def scratch(rows):
        return [
            pltpu.VMEM((8, rows), F32),
            pltpu.VMEM((3, 8, rows), F32),
            pltpu.SemaphoreType.DMA((3,)),
            pltpu.SemaphoreType.DMA((3,)),
        ]

    def __init__(self, team, mine, came, send, recv):
        self.team, self.mine, self.came = team, mine, came
        self.copies = [
            team.copy(mine, came.at[i], send.at[i], recv.at[i], other)
            for i, other in enumerate((team.sibling, team.across, team.far))
        ]

    def start(self, first, second):
        rows = first.shape[0]
        lane = lax.broadcasted_iota(jnp.int32, (rows, 128), 1)
        both = jnp.where(lane == 0, first, jnp.where(lane == 1, second, 0.0))
        self.mine[...] = jnp.transpose(both)[:8]
        for copy in self.copies:
            copy.start()

    def finish(self):
        for copy in self.copies:
            copy.wait()
        total = self.mine[...] + self.came[0] + (self.came[1] + self.came[2])
        rows = total.shape[1]
        wide = jnp.transpose(jnp.concatenate([total] * 16, axis=0))
        return wide[:, 0:1], wide[:, 1:2]


def turn(field, cosine, sine):
    return field * cosine + pltpu.roll(field, HEAD // 2, 1) * sine


def head_probs(queries, keys, length):
    rows = queries.shape[0]
    scores = right_inner(queries, keys) * (1.0 / math.sqrt(HEAD))
    row = lax.broadcasted_iota(jnp.int32, (rows, rows), 0)
    column = lax.broadcasted_iota(jnp.int32, (rows, rows), 1)
    masked = jnp.where((column <= row) & (column < length), scores, -1e30)
    expo = jnp.exp(masked - jnp.max(masked, axis=-1, keepdims=True))
    return expo / jnp.sum(expo, axis=-1, keepdims=True)


def row_sum(field):
    return jnp.sum(field, axis=-1, keepdims=True)


def over_rows(count, step, work):
    def one(i, carry):
        work(pl.ds(pl.multiple_of(i * step, step), step))
        return carry

    lax.fori_loop(0, count // step, one, 0)


def attend_kernel(
    length_ref,
    hidden,
    mine_hidden,
    q_weight,
    k_weight,
    v_weight,
    o_weight,
    q_gain,
    k_gain,
    cosine,
    sine,
    a_gain,
    q_raw,
    k_raw,
    queries,
    keys,
    values,
    scales,
    mix,
    branch,
    mid_low,
    weights,
    out_weight,
    load,
    *scratch,
):
    team = Team()
    sums = RowSums(team, *scratch[0:4])
    reduce = Reduce(team, *scratch[4:10])
    gather = Gather(team, mid_low, *scratch[10:12])
    loads = [
        pltpu.make_async_copy(source, weights.at[i], load.at[i])
        for i, source in enumerate((q_weight, k_weight, v_weight))
    ] + [pltpu.make_async_copy(o_weight, out_weight, load.at[3])]
    for one in loads:
        one.start()
    team.meet(team.sibling, team.across, team.far)
    rows, local = mix.shape
    width = mid_low.shape[1]
    length = length_ref[0]

    def project(i):
        loads[i].wait()
        return matmul(hidden[...], weights[i])

    q = project(0)
    q_raw[...] = q
    k = project(1)
    k_raw[...] = k
    sums.start(row_sum(q * q), row_sum(k * k))
    values[...] = project(2).astype(BF16)
    q_total, k_total = sums.finish()
    q_scale = lax.rsqrt(q_total * (1.0 / D) + EPS)
    k_scale = lax.rsqrt(k_total * (1.0 / D) + EPS)
    lane = lax.broadcasted_iota(jnp.int32, (rows, 128), 1)
    scales[...] = jnp.where(lane == 0, q_scale, k_scale)
    for head in range(local // HEAD):
        at = pl.ds(head * HEAD, HEAD)
        q = turn(q_raw[:, at] * q_scale * q_gain[:, at], cosine[...], sine[...]).astype(BF16)
        k = turn(k_raw[:, at] * k_scale * k_gain[:, at], cosine[...], sine[...]).astype(BF16)
        queries[:, at] = q
        keys[:, at] = k
        probs = head_probs(q, k, length).astype(BF16)
        mix[:, at] = matmul(probs, values[:, at]).astype(BF16)
    loads[3].wait()

    def make(at):
        reduce.partial[:, at] = matmul(mix[...], out_weight[:, at]).astype(BF16)

    reduce.run(make)
    shard = reduce.shard

    def norm(at):
        part = reduce.total[at, :]
        branch[at, :] = part
        unit = part * lax.rsqrt(row_sum(part * part) * (1.0 / D) + EPS)
        mid = mine_hidden[at, :].astype(F32) + a_gain[...] * unit
        whole_at = pl.ds(pl.multiple_of(team.slot * shard + at.start, at.size), at.size)
        mid_low[whole_at, :] = mid.astype(BF16)

    over_rows(shard, 16, norm)
    gather.start()
    gather.half()
    gather.finish()


ANY = pl.BlockSpec(memory_space=pl.ANY)
ON_CHIP = pl.BlockSpec(memory_space=pltpu.VMEM)
SCALAR = pl.BlockSpec(memory_space=pltpu.SMEM)


def shaped(*pairs):
    return tuple(jax.ShapeDtypeStruct(shape, kind) for shape, kind in pairs)


def attend(length, hidden, mine_hidden, weights, gains, cosine, sine, a_gain):
    rows, width = hidden.shape
    local = weights[0].shape[1]
    shard = rows // SLOTS
    return pl.pallas_call(
        attend_kernel,
        out_shape=shaped(
            ((rows, local), F32),
            ((rows, local), F32),
            ((rows, local), BF16),
            ((rows, local), BF16),
            ((rows, local), BF16),
            ((rows, 128), F32),
            ((rows, local), BF16),
            ((shard, width), F32),
            ((rows, width), BF16),
        ),
        in_specs=[SCALAR, ON_CHIP, ON_CHIP] + [ANY] * 4 + [ON_CHIP] * 5,
        out_specs=(ON_CHIP,) * 9,
        scratch_shapes=[
            pltpu.VMEM((3, width, local), BF16),
            pltpu.VMEM((local, width), BF16),
            pltpu.SemaphoreType.DMA((4,)),
        ]
        + RowSums.scratch(rows)
        + Reduce.scratch(rows, width)
        + Gather.scratch,
        compiler_params=pltpu.CompilerParams(
            collective_id=0, has_side_effects=True, vmem_limit_bytes=VMEM_CAP
        ),
        name="attend",
    )(length, hidden, mine_hidden, *weights, *gains, cosine, sine, a_gain)


def settle_kernel(
    length_ref,
    partial_in,
    mine_hidden,
    branch,
    grad_in,
    a_gain,
    m_gain,
    layer,
    d_mlp,
    m_gain_part,
    squares,
    *scratch,
):
    team = Team()
    reduce = Reduce(team, *scratch[0:6])
    gather = Gather(team, d_mlp, *scratch[6:8])
    team.meet(team.sibling, team.across)

    def make(at):
        reduce.partial[:, at] = partial_in[:, at]

    reduce.run(make)
    shard = reduce.shard
    length = length_ref[0]
    m_gain_part[...] = jnp.zeros_like(m_gain_part)
    squares[...] = jnp.zeros_like(squares)

    def folded(field):
        return sum([field[8 * i : 8 * i + 8] for i in range(field.shape[0] // 8)])

    def norm(at):
        part = reduce.total[at, :]
        scale = lax.rsqrt(row_sum(part * part) * (1.0 / D) + EPS)
        unit = part * scale
        base = branch[at, :]
        a_unit = base * lax.rsqrt(row_sum(base * base) * (1.0 / D) + EPS)
        attn_out = a_gain[...] * a_unit
        mlp_out = m_gain[...] * unit
        rows_f = mine_hidden[at, :].astype(F32)
        row = team.slot * shard + at.start + lax.broadcasted_iota(jnp.int32, (at.size, 1), 0)
        live = row < length
        layer[at, :] = jnp.where(live, rows_f + attn_out + mlp_out, 0.0).astype(BF16)
        grad = jnp.where(live, grad_in[at, :].astype(F32), 0.0)
        m_gain_part[...] += folded(grad * unit)
        for i, field in enumerate((rows_f, attn_out, mlp_out)):
            squares[i] += folded(jnp.where(live, field * field, 0.0))
        scaled = grad * m_gain[...]
        back = scale * (scaled - unit * (row_sum(scaled * unit) * (1.0 / D)))
        whole_at = pl.ds(pl.multiple_of(team.slot * shard + at.start, at.size), at.size)
        d_mlp[whole_at, :] = back.astype(BF16)

    over_rows(shard, 16, norm)
    gather.start()
    gather.half()
    gather.finish()


def settle(length, partial, mine_hidden, branch, grad_in, a_gain, m_gain):
    rows, width = partial.shape
    shard = rows // SLOTS
    return pl.pallas_call(
        settle_kernel,
        out_shape=shaped(
            ((shard, width), BF16),
            ((rows, width), BF16),
            ((8, width), F32),
            ((3, 8, width), F32),
        ),
        in_specs=[SCALAR] + [ON_CHIP] * 6,
        out_specs=(ON_CHIP,) * 4,
        scratch_shapes=Reduce.scratch(rows, width) + Gather.scratch,
        compiler_params=pltpu.CompilerParams(
            collective_id=1, has_side_effects=True, vmem_limit_bytes=VMEM_CAP
        ),
        name="settle",
    )(length, partial, mine_hidden, branch, grad_in, a_gain, m_gain)


def unattend_kernel(
    length_ref,
    partial_in,
    branch,
    grad_in,
    a_gain,
    o_weight,
    q_raw,
    k_raw,
    queries,
    keys,
    values,
    scales,
    q_gain,
    k_gain,
    cosine,
    sine,
    d_mid,
    a_gain_part,
    d_branch,
    d_heads,
    q_gain_part,
    k_gain_part,
    out_weight,
    d_mix,
    d_q,
    d_k,
    load,
    *scratch,
):
    team = Team()
    sums = RowSums(team, *scratch[0:4])
    reduce = Reduce(team, *scratch[4:10])
    gather = Gather(team, d_branch, *scratch[10:12])
    fetch = pltpu.make_async_copy(o_weight, out_weight, load.at[0])
    fetch.start()
    team.meet(team.sibling, team.across, team.far)
    rows, local = queries.shape

    def make(at):
        reduce.partial[:, at] = partial_in[:, at]

    reduce.run(make)
    shard = reduce.shard
    length = length_ref[0]
    a_gain_part[...] = jnp.zeros_like(a_gain_part)

    def norm(at):
        row = team.slot * shard + at.start + lax.broadcasted_iota(jnp.int32, (at.size, 1), 0)
        grad = jnp.where(row < length, grad_in[at, :].astype(F32), 0.0) + reduce.total[at, :]
        d_mid[at, :] = grad
        base = branch[at, :]
        scale = lax.rsqrt(row_sum(base * base) * (1.0 / D) + EPS)
        unit = base * scale
        product = grad * unit
        a_gain_part[...] += sum([product[8 * i : 8 * i + 8] for i in range(at.size // 8)])
        scaled = grad * a_gain[...]
        back = scale * (scaled - unit * (row_sum(scaled * unit) * (1.0 / D)))
        whole_at = pl.ds(pl.multiple_of(team.slot * shard + at.start, at.size), at.size)
        d_branch[whole_at, :] = back.astype(BF16)

    over_rows(shard, 16, norm)
    gather.start()
    gather.half()
    gather.finish()
    fetch.wait()
    d_mix[...] = right_inner(d_branch[...], out_weight[...]).astype(BF16)
    q_scale = scales[:, 0:1]
    k_scale = scales[:, 1:2]
    q_inner = jnp.zeros((rows, 1), F32)
    k_inner = jnp.zeros((rows, 1), F32)
    shrink = 1.0 / math.sqrt(HEAD)
    for head in range(local // HEAD):
        at = pl.ds(head * HEAD, HEAD)
        q, k, v, back = queries[:, at], keys[:, at], values[:, at], d_mix[:, at]
        probs = head_probs(q, k, length)
        d_probs = right_inner(back, v)
        d_scores = (probs * (d_probs - row_sum(probs * d_probs))).astype(BF16)
        d_heads[:, pl.ds(2 * local + head * HEAD, HEAD)] = left_inner(
            probs.astype(BF16), back
        ).astype(BF16)
        d_q_hat = turn(matmul(d_scores, k) * shrink, cosine[...], -sine[...])
        d_k_hat = turn(left_inner(d_scores, q) * shrink, cosine[...], -sine[...])
        q_unit = q_raw[:, at] * q_scale
        k_unit = k_raw[:, at] * k_scale
        q_gain_part[:, at] = jnp.sum(d_q_hat * q_unit, axis=0, keepdims=True)
        k_gain_part[:, at] = jnp.sum(d_k_hat * k_unit, axis=0, keepdims=True)
        q_scaled = d_q_hat * q_gain[:, at]
        k_scaled = d_k_hat * k_gain[:, at]
        d_q[:, at] = q_scaled
        d_k[:, at] = k_scaled
        q_inner += row_sum(q_scaled * q_unit)
        k_inner += row_sum(k_scaled * k_unit)
    sums.start(q_inner, k_inner)
    q_inner, k_inner = sums.finish()
    for i, (grad, raw, scale, inner) in enumerate(
        ((d_q, q_raw, q_scale, q_inner), (d_k, k_raw, k_scale, k_inner))
    ):
        factor = scale * scale * inner * (1.0 / D)
        d_heads[:, pl.ds(i * local, local)] = (scale * grad[...] - raw[...] * factor).astype(BF16)


def unattend(
    length, partial, branch, grad_in, a_gain, o_weight, kept, gains, cosine, sine
):
    rows, width = partial.shape
    local = o_weight.shape[0]
    shard = rows // SLOTS
    return pl.pallas_call(
        unattend_kernel,
        out_shape=shaped(
            ((shard, width), F32),
            ((8, width), F32),
            ((rows, width), BF16),
            ((rows, 3 * local), BF16),
            ((1, local), F32),
            ((1, local), F32),
        ),
        in_specs=[SCALAR] + [ON_CHIP] * 4 + [ANY] + [ON_CHIP] * 10,
        out_specs=(ON_CHIP,) * 6,
        scratch_shapes=[
            pltpu.VMEM((local, width), BF16),
            pltpu.VMEM((rows, local), BF16),
            pltpu.VMEM((rows, local), F32),
            pltpu.VMEM((rows, local), F32),
            pltpu.SemaphoreType.DMA((1,)),
        ]
        + RowSums.scratch(rows)
        + Reduce.scratch(rows, width)
        + Gather.scratch,
        compiler_params=pltpu.CompilerParams(
            collective_id=2, has_side_effects=True, vmem_limit_bytes=VMEM_CAP
        ),
        name="unattend",
    )(length, partial, branch, grad_in, a_gain, o_weight, *kept, *gains, cosine, sine)


class Deal:
    def __init__(self, count, shard, width):
        self.count = count
        self.columns = max(128, width // count)
        self.across = width // self.columns
        self.rows = shard * self.across // count

    def at(self, chunk, base=0):
        return (
            at_rows(base + (chunk // self.across) * self.rows, self.rows),
            at_rows((chunk % self.across) * self.columns, self.columns),
        )


def finish_kernel(
    length_ref,
    inverse,
    partial_in,
    d_mid,
    layer,
    layer_out,
    input_grad,
    closed,
    parked,
    leaving,
    deal_send,
    deal_recv,
    *scratch,
):
    team = Team()
    reduce = Reduce(team, *scratch[0:6])
    gathers = [
        Gather(team, whole, *scratch[6 + 2 * i : 8 + 2 * i])
        for i, whole in enumerate((layer_out, input_grad))
    ]
    count = lax.axis_size("dp")
    shard, width = d_mid.shape
    deal = Deal(count, shard, width)
    barrier = pltpu.get_barrier_semaphore()
    for step in range(1, count):
        pl.semaphore_signal(
            barrier, inc=1, device_id=(lax.rem(team.row + step, count), team.me), device_id_type=AT
        )
    for other in (team.sibling, team.across):
        pl.semaphore_signal(barrier, inc=1, device_id=(team.row, other), device_id_type=AT)
    pl.semaphore_wait(barrier, count + 1)

    def make(at):
        reduce.partial[:, at] = partial_in[:, at]

    reduce.run(make)
    length = length_ref[0]

    def close(at):
        row = team.slot * shard + at.start + lax.broadcasted_iota(jnp.int32, (at.size, 1), 0)
        closed[at, :] = jnp.where(row < length, reduce.total[at, :] + d_mid[at, :], 0.0).astype(BF16)

    over_rows(shard, 16, close)

    def send(phase, step, i, source, target):
        return pltpu.make_async_remote_copy(
            src_ref=source,
            dst_ref=target,
            send_sem=deal_send.at[phase, step, i],
            recv_sem=deal_recv.at[phase, step, i],
            device_id=(lax.rem(team.row + step, count), team.me),
            device_id_type=AT,
        )

    first = []
    for i, source in enumerate((layer, closed)):
        for step in range(1, count):
            other = lax.rem(team.row + step, count)
            copy = send(0, step, i, source.at[deal.at(other)], parked.at[team.row, i])
            copy.start()
            first.append(copy)
        parked[team.row, i] = source[deal.at(team.row)]
    for copy in first:
        copy.wait()
    mine = team.slot * shard
    second = []
    for i, target in enumerate((layer_out, input_grad)):
        for step in range(1, count):
            other = lax.rem(team.row + step, count)
            leaving[other, i] = parked[inverse[other], i]
            copy = send(1, step, i, leaving.at[other, i], target.at[deal.at(team.row, mine)])
            copy.start()
            second.append(copy)
        target[deal.at(team.row, mine)] = parked[inverse[team.row], i]
    for copy in second:
        copy.wait()
    for gather in gathers:
        gather.start()
    for gather in gathers:
        gather.half()
    for gather in gathers:
        gather.finish()


def close_layer(length, inverse, partial, d_mid, layer):
    rows, width = partial.shape
    shard = rows // SLOTS
    count = lax.axis_size("dp")
    deal = Deal(count, shard, width)
    chunk = (count, 2, deal.rows, deal.columns)
    return pl.pallas_call(
        finish_kernel,
        out_shape=shaped(((rows, width), BF16), ((rows, width), BF16)),
        in_specs=[SCALAR, SCALAR] + [ON_CHIP] * 3,
        out_specs=(ON_CHIP,) * 2,
        scratch_shapes=[
            pltpu.VMEM((shard, width), BF16),
            pltpu.VMEM(chunk, BF16),
            pltpu.VMEM(chunk, BF16),
            pltpu.SemaphoreType.DMA((2, count, 2)),
            pltpu.SemaphoreType.DMA((2, count, 2)),
        ]
        + Reduce.scratch(rows, width)
        + Gather.scratch * 2,
        compiler_params=pltpu.CompilerParams(
            collective_id=3, has_side_effects=True, vmem_limit_bytes=VMEM_CAP
        ),
        name="close_layer",
    )(length, inverse, partial, d_mid, layer)


SPLIT = 4
STEP = 256


class Wires:
    def __init__(self, send, recv):
        self.send, self.recv, self.used = send, recv, 0

    def book(self, number=1):
        self.used += number
        assert self.used <= self.send.shape[0]
        return self.used - number

    def copy(self, source, target, device, index):
        return pltpu.make_async_remote_copy(
            src_ref=source,
            dst_ref=target,
            send_sem=self.send.at[index],
            recv_sem=self.recv.at[index],
            device_id=device,
            device_id_type=AT,
        )


class Spread:
    def __init__(self, wires, grid, team, source, field):
        shard = source.shape[0] // SLOTS
        mine = at_rows(team.slot * shard, shard)
        half = at_rows(team.core * 2 * shard, 2 * shard)
        self.hops, self.sides, self.pairs = {}, {}, {}
        for step in range(1, grid.groups):
            group = lax.rem(grid.group + step, grid.groups)
            block = field.at[step]
            self.hops[step] = wires.copy(
                source.at[mine],
                block.at[mine],
                (group * grid.lanes + grid.lane, team.me),
                wires.book(),
            )
            self.sides[step] = wires.copy(
                block.at[mine], block.at[mine], (team.row, team.across), wires.book()
            )
            self.pairs[step] = wires.copy(
                block.at[half], block.at[half], (team.row, team.sibling), wires.book()
            )
        near = sorted(self.hops, key=lambda step: min(step, grid.groups - step))
        self.plan = {"hop": list(near), "side": list(near), "pair": list(near)}

    def start(self):
        for step in self.plan["hop"]:
            self.hops[step].start()

    def side(self, number=1):
        for step in self.plan["side"][:number]:
            self.hops[step].wait_recv()
            self.sides[step].start()
        del self.plan["side"][:number]

    def pair(self, number=1):
        for step in self.plan["pair"][:number]:
            self.sides[step].wait_recv()
            self.pairs[step].start()
        del self.plan["pair"][:number]

    def drain(self):
        self.side(len(self.hops))
        self.pair(len(self.hops))
        for step in self.hops:
            self.hops[step].wait_send()
            self.sides[step].wait_send()
            self.pairs[step].wait()


def silu_parts(gate, upper):
    sig = jax.nn.sigmoid(gate)
    return sig, (gate * sig * upper).astype(BF16)


def silu_back(gate, upper, sig, d_inner):
    d_gate = (d_inner * upper * sig * (1.0 + gate * (1.0 - sig))).astype(BF16)
    return d_gate, (d_inner * gate * sig).astype(BF16)


def head_back(q, k, v, back, cosine, sine, length):
    probs = head_probs(q, k, length)
    low = probs.astype(BF16)
    mix = matmul(low, v).astype(BF16)
    d_probs = right_inner(back, v)
    d_scores = (probs * (d_probs - row_sum(probs * d_probs))).astype(BF16)
    shrink = 1.0 / math.sqrt(HEAD)
    return (
        mix,
        left_inner(low, back).astype(BF16),
        turn(matmul(d_scores, k) * shrink, cosine, -sine),
        turn(left_inner(d_scores, q) * shrink, cosine, -sine),
    )


def folded(field):
    return sum([field[8 * i : 8 * i + 8] for i in range(field.shape[0] // 8)])


def layer_kernel(names, *refs):
    m = types.SimpleNamespace(**dict(zip(names, refs, strict=True)))
    team, grid = Team(), Grid(lax.axis_size("dp"))
    wires = Wires(m.wire_send, m.wire_recv)
    count, groups, lanes = grid.count, grid.groups, grid.lanes
    rows, width = m.hid.shape
    local, hidden = m.mix.shape[1], m.gate.shape[1]
    shard, strip, tile = rows // SLOTS, width // groups, width // count
    every = groups * rows
    me = team.row

    loads = {}

    def load(name, source, target):
        loads[name] = pltpu.make_async_copy(source, target, m.load.at[len(loads)])
        loads[name].start()

    load("hid", m.hidden_in, m.hid)
    load("q", m.q_weight, m.qkv.at[0])
    load("k", m.k_weight, m.qkv.at[1])
    load("v", m.v_weight, m.qkv.at[2])
    load("grad", m.upstream.at[at_rows(team.slot * shard, shard)], m.closed)
    load("o", m.o_weight, m.wo)
    load("g", m.g_weight, m.wg)
    load("u", m.u_weight, m.wu)
    load("d", m.d_weight, m.wd)

    def peer(step):
        return lax.rem(me + step, count)

    barrier = pltpu.get_barrier_semaphore()
    for step in range(1, count):
        pl.semaphore_signal(barrier, inc=1, device_id=(peer(step), team.me), device_id_type=AT)
    for other in (team.sibling, team.across, team.far):
        pl.semaphore_signal(barrier, inc=1, device_id=(me, other), device_id_type=AT)
    pl.semaphore_wait(barrier, count + 2)

    length = m.lengths[m.order[me]]

    def holder(sequence):
        found = jnp.int32(0)
        for place in range(count):
            found = jnp.where(m.order[place] == sequence, place, found)
        return found

    following = (lax.rem(grid.group + 1, groups) * lanes + grid.lane, team.me)
    sums = RowSums(team, m.sum_mine, m.sum_came, m.sum_send, m.sum_recv)
    deal = Deal(count, shard, width)

    loads["grad"].wait()
    dealt = wires.book(2 * count)
    first = []
    for step in range(1, count):
        copy = wires.copy(
            m.closed.at[deal.at(peer(step))],
            m.back_parked.at[me, 0],
            (peer(step), team.me),
            dealt + step,
        )
        copy.start()
        first.append(copy)
    m.back_parked[me, 0] = m.closed[deal.at(me)]

    loads["hid"].wait()
    hid_spread = Spread(wires, grid, team, m.hid, m.hid_all)
    hid_spread.start()

    loads["q"].wait()
    q = matmul(m.hid[...], m.qkv[0])
    m.q_raw[...] = q
    loads["k"].wait()
    k = matmul(m.hid[...], m.qkv[1])
    m.k_raw[...] = k
    sums.start(row_sum(q * q), row_sum(k * k))
    loads["v"].wait()
    m.values[...] = matmul(m.hid[...], m.qkv[2]).astype(BF16)
    q_total, k_total = sums.finish()
    q_scale = lax.rsqrt(q_total * (1.0 / D) + EPS)
    k_scale = lax.rsqrt(k_total * (1.0 / D) + EPS)
    lane = lax.broadcasted_iota(jnp.int32, (rows, 128), 1)
    m.scales[...] = jnp.where(lane == 0, q_scale, k_scale)

    def attend_head(head, carry):
        at = at_rows(head * HEAD, HEAD)
        q = turn(m.q_raw[:, at] * q_scale * m.q_gain[:, at], m.cosine[...], m.sine[...]).astype(BF16)
        k = turn(m.k_raw[:, at] * k_scale * m.k_gain[:, at], m.cosine[...], m.sine[...]).astype(BF16)
        m.queries[:, at] = q
        m.keys[:, at] = k
        probs = head_probs(q, k, length).astype(BF16)
        m.mix[:, at] = matmul(probs, m.values[:, at]).astype(BF16)
        return carry

    lax.fori_loop(0, local // HEAD, attend_head, 0)

    for copy in first:
        copy.wait()
    for step in range(1, count):
        m.back_leaving[peer(step), 0] = m.back_parked[m.order[peer(step)], 0]
    m.grad_in[deal.at(me)] = m.back_parked[m.order[me], 0]
    second = []
    for step in range(1, count):
        copy = wires.copy(
            m.back_leaving.at[peer(step), 0],
            m.grad_in.at[deal.at(me)],
            (peer(step), team.me),
            dealt + count + step,
        )
        copy.start()
        second.append(copy)

    reduce = Reduce(
        team, m.partial, m.came, m.gone, m.total, m.reduce_send, m.reduce_recv
    )

    def gather(whole, number):
        return Gather(team, whole, m.gather_send.at[number], m.gather_recv.at[number])

    loads["o"].wait()

    def make_branch(at):
        m.partial[:, at] = matmul(m.mix[...], m.wo[:, at]).astype(BF16)

    reduce.run(make_branch)
    own = m.mid_all.at[0]

    def whole_at(at):
        return pl.ds(pl.multiple_of(team.slot * shard + at.start, at.size), at.size)

    def norm_mid(at):
        part = m.total[at, :]
        m.branch[at, :] = part
        unit = part * lax.rsqrt(row_sum(part * part) * (1.0 / D) + EPS)
        mid = m.hid[whole_at(at), :].astype(F32) + m.a_gain[...] * unit
        m.mid_all[0, whole_at(at), :] = mid.astype(BF16)

    over_rows(shard, 16, norm_mid)
    mid_gather = gather(own, 0)
    mid_gather.start()
    mid_spread = Spread(wires, grid, team, own, m.mid_all)
    mid_spread.start()
    mid_gather.half()
    mid_gather.finish()
    hid_spread.side(groups)

    loads["g"].wait()
    loads["u"].wait()

    def widen(i, carry):
        at = at_rows(i * STEP, STEP)
        gate = matmul(m.mid_all[0], m.wg[:, at])
        upper = matmul(m.mid_all[0], m.wu[:, at])
        m.gate[:, at] = gate.astype(BF16)
        m.upper[:, at] = upper.astype(BF16)
        m.inner[:, at] = silu_parts(gate, upper)[1]
        return carry

    lax.fori_loop(0, hidden // STEP, widen, 0)
    loads["d"].wait()

    def make_mlp(at):
        m.partial[:, at] = matmul(m.inner[...], m.wd[:, at]).astype(BF16)

    for copy in second:
        copy.wait()
    reduce.run(make_mlp)
    m.stats[...] = jnp.zeros_like(m.stats)
    m.fold[...] = jnp.zeros_like(m.fold)

    def norm_mlp(at):
        part = m.total[at, :]
        scale = lax.rsqrt(row_sum(part * part) * (1.0 / D) + EPS)
        unit = part * scale
        base = m.branch[at, :]
        a_unit = base * lax.rsqrt(row_sum(base * base) * (1.0 / D) + EPS)
        attn_out = m.a_gain[...] * a_unit
        mlp_out = m.m_gain[...] * unit
        rows_f = m.hid[whole_at(at), :].astype(F32)
        row = team.slot * shard + at.start + lax.broadcasted_iota(jnp.int32, (at.size, 1), 0)
        live = row < length
        m.layer[at, :] = jnp.where(live, rows_f + attn_out + mlp_out, 0.0).astype(BF16)
        grad = jnp.where(live, m.grad_in[at, :].astype(F32), 0.0)
        m.fold[0] += folded(grad * unit)
        for i, field in enumerate((rows_f, attn_out, mlp_out)):
            m.fold[i + 1] += folded(jnp.where(live, field * field, 0.0))
        scaled = grad * m.m_gain[...]
        back = scale * (scaled - unit * (row_sum(scaled * unit) * (1.0 / D)))
        m.dm_all[0, whole_at(at), :] = back.astype(BF16)

    over_rows(shard, 16, norm_mlp)
    own_back = m.dm_all.at[0]
    dm_gather = gather(own_back, 1)
    dm_gather.start()
    dm_spread = Spread(wires, grid, team, own_back, m.dm_all)
    dm_spread.start()
    dm_gather.half()
    m.stats[0:1, :] = jnp.sum(m.fold[0], axis=0, keepdims=True)
    for i in range(3):
        m.stats[3 + i : 4 + i, :] = jnp.sum(m.fold[i + 1], axis=0, keepdims=True)
    dm_gather.finish()
    hid_spread.pair(groups)
    mid_spread.side(groups)

    def narrow(i, carry):
        at = at_rows(i * STEP, STEP)
        d_inner = right_inner(m.dm_all[0], m.wd[at, :])
        gate = m.gate[:, at].astype(F32)
        upper = m.upper[:, at].astype(F32)
        m.gate[:, at], m.upper[:, at] = silu_back(gate, upper, jax.nn.sigmoid(gate), d_inner)
        return carry

    lax.fori_loop(0, hidden // STEP, narrow, 0)

    def make_d_mid(at):
        m.partial[:, at] = (
            right_inner(m.gate[...], m.wg[at, :]) + right_inner(m.upper[...], m.wu[at, :])
        ).astype(BF16)

    reduce.run(make_d_mid)
    m.fold[0] = jnp.zeros_like(m.fold[0])

    def norm_d_mid(at):
        row = team.slot * shard + at.start + lax.broadcasted_iota(jnp.int32, (at.size, 1), 0)
        grad = jnp.where(row < length, m.grad_in[at, :].astype(F32), 0.0) + m.total[at, :]
        m.d_mid[at, :] = grad
        base = m.branch[at, :]
        scale = lax.rsqrt(row_sum(base * base) * (1.0 / D) + EPS)
        unit = base * scale
        m.fold[0] += folded(grad * unit)
        scaled = grad * m.a_gain[...]
        back = scale * (scaled - unit * (row_sum(scaled * unit) * (1.0 / D)))
        m.d_branch[whole_at(at), :] = back.astype(BF16)

    over_rows(shard, 16, norm_d_mid)
    d_gather = gather(m.d_branch, 2)
    d_gather.start()
    m.stats[1:2, :] = jnp.sum(m.fold[0], axis=0, keepdims=True)
    d_gather.half()
    d_gather.finish()
    dm_spread.side(2)
    mid_spread.pair(groups)
    branch_spread = Spread(wires, grid, team, m.d_branch, m.branch_all)
    branch_spread.start()

    d_mix = m.partial.at[:, pl.ds(0, local)]
    d_mix[...] = right_inner(m.d_branch[...], m.wo[...]).astype(BF16)
    q_inner = jnp.zeros((rows, 1), F32)
    k_inner = jnp.zeros((rows, 1), F32)
    q_scale = m.scales[:, 0:1]
    k_scale = m.scales[:, 1:2]

    def unattend_head(head, carry):
        at = at_rows(head * HEAD, HEAD)
        _, d_v, d_q_hat, d_k_hat = head_back(
            m.queries[:, at],
            m.keys[:, at],
            m.values[:, at],
            d_mix[:, at],
            m.cosine[...],
            m.sine[...],
            length,
        )
        m.d_heads[:, at_rows(2 * local + head * HEAD, HEAD)] = d_v
        q_unit = m.q_raw[:, at] * q_scale
        k_unit = m.k_raw[:, at] * k_scale
        m.stats[2:3, at] = jnp.sum(d_q_hat * q_unit, axis=0, keepdims=True)
        m.stats[2:3, at_rows(local + head * HEAD, HEAD)] = jnp.sum(
            d_k_hat * k_unit, axis=0, keepdims=True
        )
        q_scaled = d_q_hat * m.q_gain[:, at]
        k_scaled = d_k_hat * m.k_gain[:, at]
        m.stage[0, :, at] = q_scaled
        m.stage[1, :, at] = k_scaled
        return carry[0] + row_sum(q_scaled * q_unit), carry[1] + row_sum(k_scaled * k_unit)

    q_inner, k_inner = lax.fori_loop(0, local // HEAD, unattend_head, (q_inner, k_inner))
    sums.start(q_inner, k_inner)
    dm_spread.side()
    q_inner, k_inner = sums.finish()
    for i, (raw, scale, inner) in enumerate(
        ((m.q_raw, q_scale, q_inner), (m.k_raw, k_scale, k_inner))
    ):
        factor = scale * scale * inner * (1.0 / D)
        m.d_heads[:, pl.ds(i * local, local)] = (
            scale * m.stage[i] - raw[...] * factor
        ).astype(BF16)
    m.stat_team[team.me] = m.stats[...]
    stat_at = wires.book(3 + count)
    stat_team = [
        wires.copy(m.stats, m.stat_team.at[team.me], (me, other), stat_at + i)
        for i, other in enumerate((team.sibling, team.across, team.far))
    ]
    for copy in stat_team:
        copy.start()

    def make_input(at):
        m.partial[:, at] = (
            right_inner(m.d_heads[:, 0:local], m.qkv[0, at, :])
            + right_inner(m.d_heads[:, local : 2 * local], m.qkv[1, at, :])
            + right_inner(m.d_heads[:, 2 * local : 3 * local], m.qkv[2, at, :])
        ).astype(BF16)

    reduce.begin(make_input)

    hid_spread.drain()
    mid_spread.drain()
    dm_spread.drain()
    for k in range(groups):
        m.mid_turned[:, pl.ds(k * rows, rows)] = jnp.transpose(
            m.mid_all[k, :, at_rows(grid.group * strip, strip)]
        )
    crossed = wires.book(3 * (hidden // STEP))
    crossing = (grid.group * lanes + (1 - grid.lane), team.me)

    def tile_of(lane):
        return at_rows((grid.group * lanes + lane) * tile, tile)

    def all_rows(field, columns):
        block = field[:, :, columns]
        return block.reshape(every, block.shape[2])

    def crossings(n):
        at = at_rows(n * STEP, STEP)
        spare = pl.ds(every, tile)
        return [
            wires.copy(m.wg.at[spare, at], m.x_gate.at[:, at], crossing, crossed + 3 * n),
            wires.copy(m.wu.at[spare, at], m.x_up.at[:, at], crossing, crossed + 3 * n + 1),
            wires.copy(m.wd.at[at, spare], m.x_down.at[at, :], crossing, crossed + 3 * n + 2),
        ]

    def again(n, carry):
        at = at_rows(n * STEP, STEP)

        def block_again(k, carry):
            gate = matmul(m.mid_all[k], m.wg[:, at])
            upper = matmul(m.mid_all[k], m.wu[:, at])
            d_inner = right_inner(m.dm_all[k], m.wd[at, :])
            sig, inner = silu_parts(gate, upper)
            kept = at_rows((k - 1) * rows, rows)
            m.keep[0, kept, :] = inner
            m.keep[1, kept, :], m.keep[2, kept, :] = silu_back(gate, upper, sig, d_inner)
            return carry

        lax.fori_loop(1, groups, block_again, 0)
        whole = pl.ds(rows, every - rows)
        m.wg[0:rows, at] = m.gate[:, at]
        m.wu[0:rows, at] = m.upper[:, at]
        m.wd[at, 0:rows] = jnp.transpose(m.inner[:, at])
        m.wg[whole, at] = m.keep[1]
        m.wu[whole, at] = m.keep[2]
        for k in range(1, groups):
            kept = pl.ds((k - 1) * rows, rows)
            m.wd[at, pl.ds(k * rows, rows)] = jnp.transpose(m.keep[0, kept, :])
        turned = m.mid_turned[at_rows((1 - grid.lane) * tile, tile), :]
        spare = pl.ds(every, tile)
        m.wg[spare, at] = matmul(turned, m.wg[0:every, at]).astype(BF16)
        m.wu[spare, at] = matmul(turned, m.wu[0:every, at]).astype(BF16)
        m.wd[at, spare] = matmul(m.wd[at, 0:every], all_rows(m.dm_all, tile_of(1 - grid.lane))).astype(BF16)
        for copy in crossings(n):
            copy.start()
        for place, event in events.items():
            pl.when(n == place)(event)
        return carry

    tiles = hidden // STEP
    stat_dp = [
        wires.copy(m.stats, m.stat_dp.at[me], (peer(step), team.me), stat_at + 2 + step)
        for step in range(1, count)
    ]
    returned = wires.book(4 * count)
    parked = [
        wires.copy(
            source.at[deal.at(peer(step))],
            m.back_parked.at[me, i],
            (peer(step), team.me),
            returned + i * count + step,
        )
        for step in range(1, count)
        for i, source in enumerate((m.layer, m.closed))
    ]
    placed = [
        wires.copy(
            m.back_leaving.at[peer(step), i],
            target.at[deal.at(me, team.slot * shard)],
            (peer(step), team.me),
            returned + (2 + i) * count + step,
        )
        if step
        else pltpu.make_async_copy(
            m.back_leaving.at[me, i],
            target.at[deal.at(me, team.slot * shard)],
            m.put.at[i],
        )
        for step in range(count)
        for i, target in enumerate((m.layer_out, m.input_grad))
    ]
    holders = [holder(peer(step)) for step in range(count)]
    out_gathers = [gather(m.layer_out, 3), gather(m.input_grad, 4)]

    def add_stats():
        for copy in stat_team:
            copy.wait()
        total = (m.stat_team[0] + m.stat_team[1]) + (m.stat_team[2] + m.stat_team[3])
        line = lax.broadcasted_iota(jnp.int32, total.shape, 0)
        m.stats[...] = jnp.where(line == 2, m.stats[...], total)
        m.stat_dp[me] = m.stats[...]
        for copy in stat_dp:
            copy.start()

    def close(at):
        row = team.slot * shard + at.start + lax.broadcasted_iota(jnp.int32, (at.size, 1), 0)
        m.closed[at, :] = jnp.where(row < length, m.total[at, :] + m.d_mid[at, :], 0.0).astype(BF16)

    def park():
        reduce.end()
        over_rows(shard, 16, close)
        for copy in parked:
            copy.start()
        for i, source in enumerate((m.layer, m.closed)):
            m.back_parked[me, i] = source[deal.at(me)]
        branch_spread.side(groups)

    def place():
        for copy in parked:
            copy.wait()
        for step in range(count):
            for i in range(2):
                m.back_leaving[peer(step), i] = m.back_parked[holders[step], i]
        for copy in placed:
            copy.start()

    def share():
        for copy in placed:
            copy.wait()
        for one in out_gathers:
            one.start()

    events = {
        0: add_stats,
        1: park,
        3: place,
        4: lambda: branch_spread.pair(groups),
        tiles - 2: share,
    }
    lax.fori_loop(0, tiles, again, 0)
    for one in out_gathers:
        one.half()
    def put(source, target, index):
        return pltpu.make_async_copy(source, target, m.put.at[index])

    puts = []

    def store(value, target):
        slot = len(puts) % 2
        if len(puts) >= 2:
            puts[-2].wait()
        stage = m.stage.at[slot, pl.ds(0, value.shape[0]), pl.ds(0, value.shape[1])]
        stage[...] = value
        puts.append(put(stage, target, 2 + slot))
        puts[-1].start()

    late = []

    def bring(source, target):
        copy = pltpu.make_async_copy(source, target, m.late.at[len(late)])
        copy.start()
        late.append(copy)

    for k in range(1, groups):
        bring(m.hid_all.at[k], m.mid_all.at[k])
    turned_own = m.mid_turned.at[at_rows(grid.lane * tile, tile)]
    wide = m.stage.shape[2]
    high = rows

    def narrow_stage(slot):
        return m.stage.at[slot, :, pl.ds(0, tile)]

    def flush(copies, last, i, values):
        @pl.when(i > 0)
        def _():
            for copy in copies(i - 1):
                copy.wait()

        for copy, slot, value in zip(copies(i), last, values, strict=True):
            slot[...] = value
            copy.start()

    def wide_copies(i):
        at = at_rows(i * wide, wide)
        return [put(m.stage.at[0], m.g_own.at[:, at], 2), put(m.stage.at[1], m.u_own.at[:, at], 3)]

    def wide_part(i, carry):
        at = at_rows(i * wide, wide)
        flush(
            wide_copies,
            (m.stage.at[0], m.stage.at[1]),
            i,
            [matmul(turned_own[...], weight[0:every, at]) for weight in (m.wg, m.wu)],
        )
        return carry

    lax.fori_loop(0, hidden // wide, wide_part, 0)
    for copy in wide_copies(hidden // wide - 1):
        copy.wait()

    def high_at(i, slot):
        return at_rows((2 * i + slot) * high, high)

    def high_copies(i):
        return [put(narrow_stage(slot), m.d_own.at[high_at(i, slot), :], 2 + slot) for slot in range(2)]

    def high_part(i, carry):
        right = all_rows(m.dm_all, tile_of(grid.lane))
        flush(
            high_copies,
            (narrow_stage(0), narrow_stage(1)),
            i,
            [matmul(m.wd[high_at(i, slot), 0:every], right) for slot in range(2)],
        )
        return carry

    lax.fori_loop(0, hidden // high // 2, high_part, 0)
    for copy in high_copies(hidden // high // 2 - 1):
        copy.wait()
    for one in out_gathers:
        one.finish()

    branch_spread.drain()
    for k in range(1, groups):
        bring(m.branch_all.at[k], m.dm_all.at[k])
    for copy in late[: groups - 1]:
        copy.wait()
    for k in range(groups):
        source = m.mid_all.at[k] if k else m.hid
        m.mid_turned[:, pl.ds(k * rows, rows)] = jnp.transpose(
            source[:, at_rows(grid.group * strip, strip)]
        )
    wide_sums = RowSums(
        team, m.wide_mine, m.wide_came.at[0], m.wide_send.at[0], m.wide_recv.at[0]
    )
    spare_rows = every + tile

    def project_again(k, carry):
        block = at_rows(spare_rows + (k - 1) * rows, rows)
        lane = lax.broadcasted_iota(jnp.int32, (rows, 128), 1)
        found = jnp.zeros((rows, 128), F32)
        for i in range(2):
            raw = matmul(m.mid_all[k], m.qkv[i])
            m.wu[block, pl.ds(2 * local + i * local, local)] = raw.astype(BF16)
            found = jnp.where(lane == i, row_sum(raw * raw), found)
        m.wide_inner[at_rows((k - 1) * rows, rows), :] = found
        m.wu[block, pl.ds(local, local)] = matmul(m.mid_all[k], m.qkv[2]).astype(BF16)
        return carry

    lax.fori_loop(1, groups, project_again, 0)
    wide_sums.start(m.wide_inner[:, 0:1], m.wide_inner[:, 1:2])
    for copy in late[groups - 1 :]:
        copy.wait()
    q_total, k_total = wide_sums.finish()
    lane = lax.broadcasted_iota(jnp.int32, (every - rows, 128), 1)
    m.wide_scales[...] = lax.rsqrt(jnp.where(lane == 0, q_total, k_total) * (1.0 / D) + EPS)
    m.wide_inner[...] = jnp.zeros_like(m.wide_inner)

    def attention_again(k, carry):
        back_length = m.lengths[
            m.order[lax.rem(grid.group - k + groups, groups) * lanes + grid.lane]
        ]
        block = at_rows(spare_rows + (k - 1) * rows, rows)
        inside = at_rows((k - 1) * rows, rows)
        q_scale = m.wide_scales[inside, 0:1]
        k_scale = m.wide_scales[inside, 1:2]
        d_mix[...] = right_inner(m.dm_all[k], m.wo[...]).astype(BF16)
        q_inner = jnp.zeros((rows, 1), F32)
        k_inner = jnp.zeros((rows, 1), F32)

        def head_again(head, carry):
            at = at_rows(head * HEAD, HEAD)
            q_unit = m.wu[block, at_rows(2 * local + head * HEAD, HEAD)].astype(F32) * q_scale
            k_unit = m.wu[block, at_rows(3 * local + head * HEAD, HEAD)].astype(F32) * k_scale
            mix, d_v, d_q_hat, d_k_hat = head_back(
                turn(q_unit * m.q_gain[:, at], m.cosine[...], m.sine[...]).astype(BF16),
                turn(k_unit * m.k_gain[:, at], m.cosine[...], m.sine[...]).astype(BF16),
                m.wu[block, at_rows(local + head * HEAD, HEAD)],
                d_mix[:, at],
                m.cosine[...],
                m.sine[...],
                back_length,
            )
            m.wu[block, at] = mix
            m.wg[block, at_rows(2 * local + head * HEAD, HEAD)] = d_v
            q_scaled = d_q_hat * m.q_gain[:, at]
            k_scaled = d_k_hat * m.k_gain[:, at]
            m.wg[block, at] = q_scaled.astype(BF16)
            m.wg[block, at_rows(local + head * HEAD, HEAD)] = k_scaled.astype(BF16)
            return carry[0] + row_sum(q_scaled * q_unit), carry[1] + row_sum(k_scaled * k_unit)

        q_inner, k_inner = lax.fori_loop(0, local // HEAD, head_again, (q_inner, k_inner))
        lane = lax.broadcasted_iota(jnp.int32, (rows, 128), 1)
        m.wide_inner[inside, :] = jnp.where(lane == 0, q_inner, jnp.where(lane == 1, k_inner, 0.0))
        return carry

    lax.fori_loop(1, groups, attention_again, 0)
    wide_sums = RowSums(
        team, m.wide_mine, m.wide_came.at[1], m.wide_send.at[1], m.wide_recv.at[1]
    )
    wide_sums.start(m.wide_inner[:, 0:1], m.wide_inner[:, 1:2])
    other, this = 1 - grid.lane, grid.lane
    others = pl.ds(spare_rows, every - rows)

    def lane_of(lane):
        return at_rows(grid.group * strip + lane * tile, tile)

    def o_part(lane):
        return left_inner(m.mix[...], m.d_branch[:, lane_of(lane)]) + left_inner(
            m.wu[others, 0:local],
            m.dm_all[1:groups, :, lane_of(lane)].reshape(every - rows, tile),
        )

    def heads_part(lane, at):
        turned = m.mid_turned.at[at_rows(lane * tile, tile)]
        return matmul(turned[:, 0:rows], m.d_heads[:, at]) + matmul(
            turned[:, rows:every], m.wg[others, at]
        )

    last = wires.book(4)
    finals = []
    spare = m.qkv.at[2, pl.ds(3 * tile, local), pl.ds(0, tile)]
    spare[...] = o_part(other).astype(BF16)
    finals.append(wires.copy(spare, m.x_o, crossing, last + 3))
    finals[-1].start()
    q_inner, k_inner = wide_sums.finish()
    lane = lax.broadcasted_iota(jnp.int32, (every - rows, 128), 1)
    m.wide_inner[...] = jnp.where(lane == 0, q_inner, k_inner)

    def close_heads(k, carry):
        block = at_rows(spare_rows + (k - 1) * rows, rows)
        inside = at_rows((k - 1) * rows, rows)
        for i in range(2):
            at = pl.ds(i * local, local)
            scale = m.wide_scales[inside, i : i + 1]
            factor = scale * scale * m.wide_inner[inside, i : i + 1] * (1.0 / D)
            raw = m.wu[block, pl.ds(2 * local + i * local, local)].astype(F32)
            m.wg[block, at] = (scale * m.wg[block, at].astype(F32) - raw * factor).astype(BF16)
        return carry

    lax.fori_loop(1, groups, close_heads, 0)
    for i, target in ((2, m.x_v), (0, m.x_q), (1, m.x_k)):
        spare = m.qkv.at[2, pl.ds(i * tile, tile)]
        spare[...] = heads_part(other, pl.ds(i * local, local)).astype(BF16)
        finals.append(wires.copy(spare, target, crossing, last + i))
        finals[-1].start()
    for i, target in enumerate((m.q_own, m.k_own, m.v_own)):
        store(heads_part(this, pl.ds(i * local, local)), target)
    output = o_part(this)
    for i in range(local // high):
        store(output[i * high : (i + 1) * high], m.o_own.at[pl.ds(i * high, high), :])
    for copy in puts[-2:]:
        copy.wait()

    def arrived(n, carry):
        for copy in crossings(n):
            copy.wait()
        return carry

    for copy in stat_dp:
        copy.wait()
    m.stat_out[...] = sum([m.stat_dp[i] for i in range(1, count)], m.stat_dp[0])
    lax.fori_loop(0, tiles, arrived, 0)
    for copy in finals:
        copy.wait()


def whole_layer(grid, args):
    (hidden_in, upstream, lengths, order, q_weight, k_weight, v_weight, o_weight) = args[:8]
    (q_gain, k_gain, a_gain, g_weight, u_weight, d_weight, m_gain, cosine, sine) = args[8:]
    rows, width = hidden_in.shape
    local, hidden = q_weight.shape[1], g_weight.shape[1]
    count, groups = grid.count, grid.groups
    shard, strip, tile = rows // SLOTS, width // groups, width // count
    every = groups * rows
    deal = Deal(count, shard, width)
    chunk = (deal.rows, deal.columns)
    inputs = [
        ("lengths", SCALAR, lengths),
        ("order", SCALAR, order),
        ("hidden_in", ANY, hidden_in),
        ("upstream", ANY, upstream),
        ("q_weight", ANY, q_weight),
        ("k_weight", ANY, k_weight),
        ("v_weight", ANY, v_weight),
        ("o_weight", ANY, o_weight),
        ("g_weight", ANY, g_weight),
        ("u_weight", ANY, u_weight),
        ("d_weight", ANY, d_weight),
        ("q_gain", ON_CHIP, q_gain),
        ("k_gain", ON_CHIP, k_gain),
        ("a_gain", ON_CHIP, a_gain),
        ("m_gain", ON_CHIP, m_gain),
        ("cosine", ON_CHIP, cosine),
        ("sine", ON_CHIP, sine),
    ]
    outputs = [
        ("layer_out", (rows, width), BF16),
        ("input_grad", (rows, width), BF16),
        ("g_own", (tile, hidden), F32),
        ("u_own", (tile, hidden), F32),
        ("d_own", (hidden, tile), F32),
        ("q_own", (tile, local), F32),
        ("k_own", (tile, local), F32),
        ("v_own", (tile, local), F32),
        ("o_own", (local, tile), F32),
        ("x_gate", (tile, hidden), BF16),
        ("x_up", (tile, hidden), BF16),
        ("x_down", (hidden, tile), BF16),
        ("x_q", (tile, local), BF16),
        ("x_k", (tile, local), BF16),
        ("x_v", (tile, local), BF16),
        ("x_o", (local, tile), BF16),
        ("hid_all", (groups, rows, width), BF16),
        ("branch_all", (groups, rows, width), BF16),
        ("stat_out", (8, width), F32),
    ]
    wires = 160
    scratch = [
        ("qkv", pltpu.VMEM((3, width, local), BF16)),
        ("wo", pltpu.VMEM((local, width), BF16)),
        ("wg", pltpu.VMEM((width, hidden), BF16)),
        ("wu", pltpu.VMEM((width, hidden), BF16)),
        ("wd", pltpu.VMEM((hidden, width), BF16)),
        ("hid", pltpu.VMEM((rows, width), BF16)),
        ("mid_all", pltpu.VMEM((groups, rows, width), BF16)),
        ("dm_all", pltpu.VMEM((groups, rows, width), BF16)),
        ("gate", pltpu.VMEM((rows, hidden), BF16)),
        ("upper", pltpu.VMEM((rows, hidden), BF16)),
        ("inner", pltpu.VMEM((rows, hidden), BF16)),
        ("q_raw", pltpu.VMEM((rows, local), F32)),
        ("k_raw", pltpu.VMEM((rows, local), F32)),
        ("queries", pltpu.VMEM((rows, local), BF16)),
        ("keys", pltpu.VMEM((rows, local), BF16)),
        ("values", pltpu.VMEM((rows, local), BF16)),
        ("scales", pltpu.VMEM((rows, 128), F32)),
        ("mix", pltpu.VMEM((rows, local), BF16)),
        ("d_branch", pltpu.VMEM((rows, width), BF16)),
        ("d_heads", pltpu.VMEM((rows, 3 * local), BF16)),
        ("mid_turned", pltpu.VMEM((strip, every), BF16)),
        ("keep", pltpu.VMEM((3, every - rows, STEP), BF16)),
        ("stage", pltpu.VMEM((2, rows, local), F32)),
        ("branch", pltpu.VMEM((shard, width), F32)),
        ("d_mid", pltpu.VMEM((shard, width), F32)),
        ("layer", pltpu.VMEM((shard, width), BF16)),
        ("closed", pltpu.VMEM((shard, width), BF16)),
        ("grad_in", pltpu.VMEM((shard, width), BF16)),
        ("back_parked", pltpu.VMEM((count, 2) + chunk, BF16)),
        ("back_leaving", pltpu.VMEM((count, 2) + chunk, BF16)),
        ("fold", pltpu.VMEM((4, 8, width), F32)),
        ("stats", pltpu.VMEM((8, width), F32)),
        ("stat_team", pltpu.VMEM((SLOTS, 8, width), F32)),
        ("stat_dp", pltpu.VMEM((count, 8, width), F32)),
        ("partial", pltpu.VMEM((rows, width), BF16)),
        ("came", pltpu.VMEM((3, shard, width), BF16)),
        ("gone", pltpu.VMEM((shard, width), BF16)),
        ("total", pltpu.VMEM((shard, width), F32)),
        ("sum_mine", pltpu.VMEM((8, rows), F32)),
        ("sum_came", pltpu.VMEM((3, 8, rows), F32)),
        ("wide_mine", pltpu.VMEM((8, every - rows), F32)),
        ("wide_came", pltpu.VMEM((2, 3, 8, every - rows), F32)),
        ("wide_scales", pltpu.VMEM((every - rows, 128), F32)),
        ("wide_inner", pltpu.VMEM((every - rows, 128), F32)),
        ("wide_send", pltpu.SemaphoreType.DMA((2, 3))),
        ("wide_recv", pltpu.SemaphoreType.DMA((2, 3))),
        ("sum_send", pltpu.SemaphoreType.DMA((3,))),
        ("sum_recv", pltpu.SemaphoreType.DMA((3,))),
        ("reduce_send", pltpu.SemaphoreType.DMA((3, SPLIT))),
        ("reduce_recv", pltpu.SemaphoreType.DMA((3, SPLIT))),
        ("gather_send", pltpu.SemaphoreType.DMA((5, 3))),
        ("gather_recv", pltpu.SemaphoreType.DMA((5, 3))),
        ("wire_send", pltpu.SemaphoreType.DMA((wires,))),
        ("wire_recv", pltpu.SemaphoreType.DMA((wires,))),
        ("load", pltpu.SemaphoreType.DMA((9,))),
        ("put", pltpu.SemaphoreType.DMA((4,))),
        ("late", pltpu.SemaphoreType.DMA((2 * groups,))),
    ]
    names = [entry[0] for entry in inputs + outputs + scratch]
    results = pl.pallas_call(
        functools.partial(layer_kernel, names),
        out_shape=shaped(*[entry[1:] for entry in outputs]),
        in_specs=[entry[1] for entry in inputs],
        out_specs=(ANY,) * (len(outputs) - 1) + (ON_CHIP,),
        scratch_shapes=[entry[1] for entry in scratch],
        compiler_params=pltpu.CompilerParams(
            collective_id=4, has_side_effects=True, vmem_limit_bytes=63 * 2**20
        ),
        name="whole_layer",
    )(*[entry[2] for entry in inputs])
    return dict(zip([entry[0] for entry in outputs], results, strict=True))


def body(
    hidden_in,
    upstream_grad,
    seq_lengths,
    position_order,
    query_weight,
    key_weight,
    value_weight,
    output_weight,
    query_gain,
    key_gain,
    attn_gain,
    gate_weight,
    up_weight,
    down_weight,
    mlp_gain,
):
    count = lax.axis_size("dp")
    ways = lax.axis_size("tensor")
    myself = lax.axis_index("dp")
    part = lax.axis_index("tensor")
    grid = Grid(count)
    index = jnp.arange(count, dtype=jnp.int32)
    inverse = jnp.sum(
        index[None, :] * (position_order[None, :] == index[:, None]).astype(jnp.int32), axis=1
    )
    rows = hidden_in.shape[1]
    width = hidden_in.shape[2]
    shard = rows // ways
    if grid.lanes == 2 and grid.groups * rows + width // count <= width:
        cosine, sine = rope_constants(rows, HEAD)
        found = whole_layer(
            grid,
            (
                hidden_in[0],
                upstream_grad[0],
                seq_lengths,
                position_order,
                query_weight,
                key_weight,
                value_weight,
                output_weight,
                query_gain[None],
                key_gain[None],
                attn_gain[None],
                gate_weight,
                up_weight,
                down_weight,
                mlp_gain[None],
                cosine,
                sine,
            ),
        )
        local = query_weight.shape[1]

        def joined(own, other):
            return found[own] + found[other].astype(F32)

        stats = found["stat_out"]
        squares = jnp.sum(stats[3:6], axis=1)
        return (
            found["layer_out"][None],
            found["input_grad"][None],
            joined("q_own", "x_q"),
            joined("k_own", "x_k"),
            joined("v_own", "x_v"),
            joined("o_own", "x_o"),
            stats[2, :local],
            stats[2, local : 2 * local],
            stats[1],
            joined("g_own", "x_gate"),
            joined("u_own", "x_up"),
            joined("d_own", "x_down"),
            stats[0],
            jnp.sqrt(squares / (jnp.sum(seq_lengths).astype(F32) * D)),
        )

    piece = shard // count
    seq_here = jnp.sum(jnp.where(index == myself, position_order, 0))
    length = jnp.sum(jnp.where(index == seq_here, seq_lengths, 0))[None]
    slot = part % 2 * 2 + part // 2

    def exchange(pieces):
        return lax.all_to_all(pieces, "dp", split_axis=0, concat_axis=0, tiled=True)

    def my_rows(field):
        return lax.dynamic_slice_in_dim(field, slot * shard, shard, axis=0)

    first = exchange(my_rows(upstream_grad[0]).reshape(count, piece, width))
    second = exchange(jnp.take(first, position_order, axis=0))
    grad_in = second.reshape(shard, width)

    rows_low = hidden_in[0]
    my_low = my_rows(rows_low)
    local = query_weight.shape[1]
    strip = width // grid.groups
    tile = width // count

    def strip_of(field, group):
        return lax.dynamic_slice_in_dim(field, group * strip, strip, axis=1)

    def strips(field):
        found = [strip_of(field, grid.group)]
        for step in range(1, grid.groups):
            found.append(
                grid.shift_groups(
                    strip_of(field, (grid.group + step) % grid.groups), step
                )
            )
        return jnp.concatenate(found, axis=0)

    def tile_of(field, lane):
        return lax.dynamic_slice_in_dim(field, lane * tile, tile, axis=1)

    def reduced(product, field):
        sent = []
        for step in range(1, grid.lanes):
            other = product(tile_of(field, (grid.lane + step) % grid.lanes)).astype(BF16)
            sent.append(grid.shift_lanes(other, step))
        mine = product(tile_of(field, grid.lane))
        for other in sent:
            mine = mine + other.astype(F32)
        return mine

    hidden_strips = strips(rows_low)

    cosine, sine = rope_tables(rows, HEAD)
    cosine = jnp.concatenate([cosine, cosine], axis=1)
    sine = jnp.concatenate([-sine, sine], axis=1)
    gains = (query_gain[None], key_gain[None])
    q_raw, k_raw, queries, keys, values, scales, attn_mix, branch, mid_low = attend(
        length,
        rows_low,
        my_low,
        (query_weight, key_weight, value_weight, output_weight),
        gains,
        cosine,
        sine,
        attn_gain[None],
    )
    mix_all = jnp.concatenate([attn_mix] + grid.ring(attn_mix), axis=0)
    mid_others = shared_ring(grid, mid_low)

    gate = matmul(mid_low, gate_weight)
    upper = matmul(mid_low, up_weight)
    sig = jax.nn.sigmoid(gate)
    inner = (gate * sig * upper).astype(BF16)
    layer, d_mlp, mlp_gain_part, squares = settle(
        length,
        matmul(inner, down_weight).astype(BF16),
        my_low,
        branch,
        grad_in,
        attn_gain[None],
        mlp_gain[None],
    )
    d_mlp_others = shared_ring(grid, d_mlp)

    def inner_back(gate, upper, d_mlp):
        d_inner = right_inner(d_mlp, down_weight)
        sig = jax.nn.sigmoid(gate)
        d_gate = (d_inner * upper * sig * (1.0 + gate * (1.0 - sig))).astype(BF16)
        d_up = (d_inner * gate * sig).astype(BF16)
        return d_gate, d_up

    d_gate, d_up = inner_back(gate, upper, d_mlp)
    d_mid, attn_gain_part, d_branch, d_heads, query_gain_part, key_gain_part = unattend(
        length,
        (right_inner(d_gate, gate_weight) + right_inner(d_up, up_weight)).astype(BF16),
        branch,
        grad_in,
        attn_gain[None],
        output_weight,
        (q_raw, k_raw, queries, keys, values, scales),
        gains,
        cosine,
        sine,
    )
    d_branch_strips = strips(d_branch)
    d_heads_all = jnp.concatenate([d_heads] + grid.ring(d_heads), axis=0)
    layer_out, input_grad = close_layer(
        length,
        inverse,
        (
            right_inner(d_heads[:, :local], query_weight)
            + right_inner(d_heads[:, local : 2 * local], key_weight)
            + right_inner(d_heads[:, 2 * local :], value_weight)
        ).astype(BF16),
        d_mid,
        layer,
    )

    gate_o = matmul(mid_others, gate_weight)
    upper_o = matmul(mid_others, up_weight)
    inner_o = (jax.nn.silu(gate_o) * upper_o).astype(BF16)
    d_gate_o, d_up_o = inner_back(gate_o, upper_o, d_mlp_others)

    def strip_all(own, others):
        return jnp.concatenate([strip_of(own, grid.group), strip_of(others, grid.group)], axis=0)

    mid_strips = strip_all(mid_low, mid_others)
    d_mlp_strips = strip_all(d_mlp, d_mlp_others)
    d_gate_all = jnp.concatenate([d_gate, d_gate_o], axis=0)
    d_up_all = jnp.concatenate([d_up, d_up_o], axis=0)
    inner_all = jnp.concatenate([inner, inner_o], axis=0)
    gate_part = reduced(lambda tile: left_inner(tile, d_gate_all), mid_strips)
    up_part = reduced(lambda tile: left_inner(tile, d_up_all), mid_strips)
    down_part = reduced(lambda tile: left_inner(inner_all, tile), d_mlp_strips)
    output_part = reduced(lambda tile: left_inner(mix_all, tile), d_branch_strips)
    heads_part = reduced(lambda tile: left_inner(tile, d_heads_all), hidden_strips)
    query_part = heads_part[:, :local]
    key_part = heads_part[:, local : 2 * local]
    value_part = heads_part[:, 2 * local :]

    shared = jnp.concatenate(
        [jnp.sum(attn_gain_part, axis=0), jnp.sum(mlp_gain_part, axis=0), jnp.sum(squares, axis=(1, 2))]
    )
    shared = shared + sibling(shared)
    shared = shared + across(shared)
    sums = grid.total(jnp.concatenate([shared, query_gain_part[0], key_gain_part[0]]))
    attn_gain_grad = sums[:width]
    mlp_gain_grad = sums[width : 2 * width]
    squares = sums[2 * width : 2 * width + 3]
    query_gain_grad = sums[2 * width + 3 : 2 * width + 3 + local]
    key_gain_grad = sums[2 * width + 3 + local :]
    rms_values = jnp.sqrt(squares / (jnp.sum(seq_lengths).astype(F32) * D))

    return (
        layer_out[None],
        input_grad[None],
        query_part,
        key_part,
        value_part,
        output_part,
        query_gain_grad,
        key_gain_grad,
        attn_gain_grad,
        gate_part,
        up_part,
        down_part,
        mlp_gain_grad,
        rms_values,
    )


def solution(mesh):
    placed = (
        P("dp", None, None),
        P("dp", None, None),
        P(),
        P(),
        P(None, "tensor"),
        P(None, "tensor"),
        P(None, "tensor"),
        P("tensor", None),
        P("tensor"),
        P("tensor"),
        P(),
        P(None, "tensor"),
        P(None, "tensor"),
        P("tensor", None),
        P(),
    )
    return jax.shard_map(
        body,
        mesh=mesh,
        in_specs=placed,
        out_specs=(
            P("dp", None, None),
            P("dp", None, None),
            P("dp", "tensor"),
            P("dp", "tensor"),
            P("dp", "tensor"),
            P("tensor", "dp"),
            P("tensor"),
            P("tensor"),
            P(),
            P("dp", "tensor"),
            P("dp", "tensor"),
            P("tensor", "dp"),
            P(),
            P(),
        ),
        check_vma=False,
    )
```

profile of v0, /device:TPU:0, one launch (start us, length us, event | category | flops | bytes accessed | tf_op | source)
XLA Modules:
  0.0 283.3 jit_solution(2870733476252930116)
XLA Ops:
  0.7 266.3 %whole_layer.1 = (bf16[256,2048]{1,0:T(8,128)(2,1)}, bf16[256,2048]{1,0:T(8,128)(2,1)}, f32[256,2048]{1,0:T(8,128)}, f32[256,2048]{1,0:T(8,128)}, f32[2048,256]{...) custom-call(s32[8]{0:T(128)} %refs_0_.1, ...), custom_call_target="tpu_custom_call" | custom-call | tf_op jit(solution)/shard_map/whole_layer/pallas_call | solution.py:1674
  266.9 0.0 copy-start.4
  267.0 0.0 copy-start.5
  267.0 0.0 copy-start.10
  267.0 0.0 copy-start.11
  267.0 0.0 copy-start.1
  267.0 5.8 %convert_add_fusion.1 = (f32[256,2048]{1,0:T(8,128)}, f32[256,2048]{1,0:T(8,128)}) fusion(f32[256,2048]{1,0:T(8,128)} %get-tuple-element.44, bf16[256,2048]{1,0:T(8,128)(2,1)} %get-tuple-element.45, f32[256,2048]{1,0:T(8,128)} %get-tuple-element.42, bf16[256,2048]{1,0:T(8,128)(2,1)} %get-tuple-element.43), kind=kLoop, calls=%fused_computation.1 | loop fusion | flops 2097152 | bytes 10485760 | tf_op jit(solution)/shard_map/add | solution.py:1744
  272.8 0.0 copy-done.4
  272.8 0.0 copy-done.5
  272.8 0.0 copy-done.10
  272.9 0.0 copy-done.11
  272.9 1.1 convert_add_fusion.4
  274.0 0.0 copy-done.1
  274.0 0.8 copy-done
  274.8 1.6 convert_add_fusion
  276.4 0.0 copy-done.7
  276.4 0.0 copy-done.9
  276.4 0.0 copy-start.2
  276.4 0.8 convert_add_fusion.3
  277.3 0.0 copy-done.6
  277.3 0.0 copy-done.8
  277.3 0.9 convert_add_fusion.6
  278.2 0.0 copy-done.12
  278.2 0.6 fusion
  278.8 0.6 fusion.1
  279.4 0.1 slice_reduce_fusion
  279.5 0.0 copy-done.13
  279.5 0.6 reduce_sum.19
  280.8 0.5 divide_sqrt_fusion
  281.3 0.0 copy-done.3
  281.3 1.0 copy.33
  282.3 1.0 copy.34
  (9 shorter events, 0.0 us)
Async XLA Ops:
  266.9 5.9 %copy-start.4 = (f32[256,512]{1,0:T(8,128)S(1)}, f32[256,512]{1,0:T(8,128)}, u32[]{:S(2)}) copy-start(f32[256,512]{1,0:T(8,128)} %get-tuple-element.35) | copy-start | bytes 1572868
  267.0 5.9 %copy-start.5 = (f32[256,512]{1,0:T(8,128)S(1)}, f32[256,512]{1,0:T(8,128)}, u32[]{:S(2)}) copy-start(f32[256,512]{1,0:T(8,128)} %get-tuple-element.37) | copy-start | bytes 1572868
  267.0 5.9 %copy-start.10 = (bf16[256,512]{1,0:T(8,128)(2,1)S(1)}, bf16[256,512]{1,0:T(8,128)(2,1)}, u32[]{:S(2)}) copy-start(bf16[256,512]{1,0:T(8,128)(2,1)} %get-tuple-element.36) | copy-start | bytes 786436
  267.0 5.9 %copy-start.11 = (bf16[256,512]{1,0:T(8,128)(2,1)S(1)}, bf16[256,512]{1,0:T(8,128)(2,1)}, u32[]{:S(2)}) copy-start(bf16[256,512]{1,0:T(8,128)(2,1)} %get-tuple-element.38) | copy-start | bytes 786436
  267.0 7.0 %copy-start.1 = (bf16[2048,256]{1,0:T(8,128)(2,1)S(1)}, bf16[2048,256]{1,0:T(8,128)(2,1)}, u32[]{:S(2)}) copy-start(bf16[2048,256]{1,0:T(8,128)(2,1)} %get-tuple-element.47) | copy-start | bytes 3145732
  272.8 2.0 copy-start
  274.8 1.6 copy-start.7
  274.8 1.6 copy-start.9
  274.8 2.5 copy-start.6
  274.8 2.5 copy-start.8
  276.4 1.8 copy-start.12
  276.4 3.1 %copy-start.13 = (s32[8]{0:T(128)S(1)}, s32[8]{0:T(128)}, u32[]{:S(2)}) copy-start(s32[8]{0:T(128)} %refs_0_.1) | copy-start | bytes 100
  276.4 4.9 %copy-start.3 = (bf16[256,2048]{1,0:T(8,128)(2,1)S(1)}, bf16[256,2048]{1,0:T(8,128)(2,1)}, u32[]{:S(2)}) copy-start(bf16[256,2048]{1,0:T(8,128)(2,1)} %get-tuple-element.31) | copy-start | bytes 3145732
  276.4 5.9 %copy-start.2 = (bf16[256,2048]{1,0:T(8,128)(2,1)S(1)}, bf16[256,2048]{1,0:T(8,128)(2,1)}, u32[]{:S(2)}) copy-start(bf16[256,2048]{1,0:T(8,128)(2,1)} %get-tuple-element.32) | copy-start | bytes 3145732
where the time goes:
time: 284 us; the launch traced here: 283 us
  Pallas kernels  266 us (94%)
  other arithmetic  11.6 us (4%)
  local copies, waits for them, and re-layouts  3.99 us (1%)
    pallas_call x1, Pallas kernels, whole_layer(): pl.pallas_call(functools.partial(layer_kernel, names), out_shape=shaped(*...  266 us
    add x5, other arithmetic, joined(): return found[own] + found[other].astype(F32)  10.3 us

commit v1 on v0

--- a/solution.py
+++ b/solution.py
@@ -953,8 +953,6 @@
     m.back_parked[me, 0] = m.closed[deal.at(me)]
 
     loads["hid"].wait()
-    hid_spread = Spread(wires, grid, team, m.hid, m.hid_all)
-    hid_spread.start()
 
     loads["q"].wait()
     q = matmul(m.hid[...], m.qkv[0])
@@ -1031,8 +1029,6 @@
     mid_spread.start()
     mid_gather.half()
     mid_gather.finish()
-    hid_spread.side(groups)
-
     loads["g"].wait()
     loads["u"].wait()
 
@@ -1088,8 +1084,9 @@
     for i in range(3):
         m.stats[3 + i : 4 + i, :] = jnp.sum(m.fold[i + 1], axis=0, keepdims=True)
     dm_gather.finish()
-    hid_spread.pair(groups)
     mid_spread.side(groups)
+    hid_spread = Spread(wires, grid, team, m.hid, m.hid_all)
+    hid_spread.start()
 
     def narrow(i, carry):
         at = at_rows(i * STEP, STEP)
@@ -1127,7 +1124,7 @@
     m.stats[1:2, :] = jnp.sum(m.fold[0], axis=0, keepdims=True)
     d_gather.half()
     d_gather.finish()
-    dm_spread.side(2)
+    dm_spread.side(groups)
     mid_spread.pair(groups)
     branch_spread = Spread(wires, grid, team, m.d_branch, m.branch_all)
     branch_spread.start()
@@ -1165,7 +1162,6 @@
 
     q_inner, k_inner = lax.fori_loop(0, local // HEAD, unattend_head, (q_inner, k_inner))
     sums.start(q_inner, k_inner)
-    dm_spread.side()
     q_inner, k_inner = sums.finish()
     for i, (raw, scale, inner) in enumerate(
         ((m.q_raw, q_scale, q_inner), (m.k_raw, k_scale, k_inner))
@@ -1192,7 +1188,6 @@
 
     reduce.begin(make_input)
 
-    hid_spread.drain()
     mid_spread.drain()
     dm_spread.drain()
     for k in range(groups):
@@ -1308,7 +1303,7 @@
             copy.start()
         for i, source in enumerate((m.layer, m.closed)):
             m.back_parked[me, i] = source[deal.at(me)]
-        branch_spread.side(groups)
+        hid_spread.side(groups)
 
     def place():
         for copy in parked:
@@ -1328,13 +1323,11 @@
     events = {
         0: add_stats,
         1: park,
-        3: place,
-        4: lambda: branch_spread.pair(groups),
-        tiles - 2: share,
+        tiles - 3: lambda: hid_spread.pair(groups),
+        tiles - 2: lambda: branch_spread.side(groups),
     }
     lax.fori_loop(0, tiles, again, 0)
-    for one in out_gathers:
-        one.half()
+    hid_spread.drain()
     def put(source, target, index):
         return pltpu.make_async_copy(source, target, m.put.at[index])
 
@@ -1412,13 +1405,8 @@
     lax.fori_loop(0, hidden // high // 2, high_part, 0)
     for copy in high_copies(hidden // high // 2 - 1):
         copy.wait()
-    for one in out_gathers:
-        one.finish()
-
-    branch_spread.drain()
-    for k in range(1, groups):
-        bring(m.branch_all.at[k], m.dm_all.at[k])
-    for copy in late[: groups - 1]:
+
+    for copy in late:
         copy.wait()
     for k in range(groups):
         source = m.mid_all.at[k] if k else m.hid
@@ -1444,6 +1432,11 @@
 
     lax.fori_loop(1, groups, project_again, 0)
     wide_sums.start(m.wide_inner[:, 0:1], m.wide_inner[:, 1:2])
+    branch_spread.pair(groups)
+    place()
+    branch_spread.drain()
+    for k in range(1, groups):
+        bring(m.branch_all.at[k], m.dm_all.at[k])
     for copy in late[groups - 1 :]:
         copy.wait()
     q_total, k_total = wide_sums.finish()
@@ -1539,6 +1532,7 @@
         spare[...] = heads_part(other, pl.ds(i * local, local)).astype(BF16)
         finals.append(wires.copy(spare, target, crossing, last + i))
         finals[-1].start()
+    share()
     for i, target in enumerate((m.q_own, m.k_own, m.v_own)):
         store(heads_part(this, pl.ds(i * local, local)), target)
     output = o_part(this)
@@ -1552,6 +1546,10 @@
             copy.wait()
         return carry
 
+    for one in out_gathers:
+        one.half()
+    for one in out_gathers:
+        one.finish()
     for copy in stat_dp:
         copy.wait()
     m.stat_out[...] = sum([m.stat_dp[i] for i in range(1, count)], m.stat_dp[0])

time: 284 us -> 253 us (0.89)
  Pallas kernels: 266 us -> 236 us
    pallas_call x1, Pallas kernels: 266 us -> 236 us  [whole_layer(): pl.pallas_call(functools.partial(layer_kernel, names), out_shape=shaped(*...]
where the time goes in v1:
time: 253 us
  Pallas kernels  236 us (93%)
  other arithmetic  11.6 us (5%)
  local copies, waits for them, and re-layouts  3.99 us (2%)
    pallas_call x1, Pallas kernels, whole_layer(): pl.pallas_call(functools.partial(layer_kernel, names), out_shape=shaped(*...  236 us
    add x5, other arithmetic, joined(): return found[own] + found[other].astype(F32)  10.3 us

profile of v1, /device:TPU:0, one launch (start us, length us, event | category | flops | bytes accessed | tf_op | source)
XLA Modules:
  0.0 252.6 jit_solution(7519464799664010089)
XLA Ops:
  0.7 235.6 %whole_layer.1 = (bf16[256,2048]{1,0:T(8,128)(2,1)}, bf16[256,2048]{1,0:T(8,128)(2,1)}, f32[256,2048]{1,0:T(8,128)}, f32[256,2048]{1,0:T(8,128)}, f32[2048,256]{...) custom-call(s32[8]{0:T(128)} %refs_0_.1, ...), custom_call_target="tpu_custom_call" | custom-call | tf_op jit(solution)/shard_map/whole_layer/pallas_call | solution.py:1672
  236.3 0.0 copy-start.4
  236.3 0.0 copy-start.5
  236.3 0.0 copy-start.10
  236.3 0.0 copy-start.11
  236.3 0.0 copy-start.1
  236.3 5.8 %convert_add_fusion.1 = (f32[256,2048]{1,0:T(8,128)}, f32[256,2048]{1,0:T(8,128)}) fusion(f32[256,2048]{1,0:T(8,128)} %get-tuple-element.44, bf16[256,2048]{1,0:T(8,128)(2,1)} %get-tuple-element.45, f32[256,2048]{1,0:T(8,128)} %get-tuple-element.42, bf16[256,2048]{1,0:T(8,128)(2,1)} %get-tuple-element.43), kind=kLoop, calls=%fused_computation.1 | loop fusion | flops 2097152 | bytes 10485760 | tf_op jit(solution)/shard_map/add | solution.py:1742
  242.2 0.0 copy-done.4
  242.2 0.0 copy-done.5
  242.2 0.0 copy-done.10
  242.2 0.0 copy-done.11
  242.2 1.1 convert_add_fusion.4
  243.3 0.0 copy-done.1
  243.3 0.8 copy-done
  244.2 1.6 convert_add_fusion
  245.8 0.0 copy-done.7
  245.8 0.0 copy-done.9
  245.8 0.0 copy-start.2
  245.8 0.8 convert_add_fusion.3
  246.6 0.0 copy-done.6
  246.6 0.0 copy-done.8
  246.6 0.9 convert_add_fusion.6
  247.5 0.0 copy-done.12
  247.5 0.6 fusion
  248.1 0.6 fusion.1
  248.7 0.1 slice_reduce_fusion
  248.8 0.0 copy-done.13
  248.8 0.6 reduce_sum.19
  250.1 0.5 divide_sqrt_fusion
  250.6 0.0 copy-done.3
  250.6 1.0 copy.33
  251.6 1.0 copy.34
  (9 shorter events, 0.0 us)
Async XLA Ops:
  236.3 5.9 %copy-start.4 = (f32[256,512]{1,0:T(8,128)S(1)}, f32[256,512]{1,0:T(8,128)}, u32[]{:S(2)}) copy-start(f32[256,512]{1,0:T(8,128)} %get-tuple-element.35) | copy-start | bytes 1572868
  236.3 5.9 %copy-start.5 = (f32[256,512]{1,0:T(8,128)S(1)}, f32[256,512]{1,0:T(8,128)}, u32[]{:S(2)}) copy-start(f32[256,512]{1,0:T(8,128)} %get-tuple-element.37) | copy-start | bytes 1572868
  236.3 5.9 %copy-start.10 = (bf16[256,512]{1,0:T(8,128)(2,1)S(1)}, bf16[256,512]{1,0:T(8,128)(2,1)}, u32[]{:S(2)}) copy-start(bf16[256,512]{1,0:T(8,128)(2,1)} %get-tuple-element.36) | copy-start | bytes 786436
  236.3 5.9 %copy-start.11 = (bf16[256,512]{1,0:T(8,128)(2,1)S(1)}, bf16[256,512]{1,0:T(8,128)(2,1)}, u32[]{:S(2)}) copy-start(bf16[256,512]{1,0:T(8,128)(2,1)} %get-tuple-element.38) | copy-start | bytes 786436
  236.3 7.0 %copy-start.1 = (bf16[2048,256]{1,0:T(8,128)(2,1)S(1)}, bf16[2048,256]{1,0:T(8,128)(2,1)}, u32[]{:S(2)}) copy-start(bf16[2048,256]{1,0:T(8,128)(2,1)} %get-tuple-element.47) | copy-start | bytes 3145732
  242.2 2.0 copy-start
  244.1 1.6 copy-start.7
  244.1 1.6 copy-start.9
  244.2 2.5 copy-start.6
  244.2 2.5 copy-start.8
  245.7 1.8 copy-start.12
  245.8 3.1 %copy-start.13 = (s32[8]{0:T(128)S(1)}, s32[8]{0:T(128)}, u32[]{:S(2)}) copy-start(s32[8]{0:T(128)} %refs_0_.1) | copy-start | bytes 100
  245.8 4.9 %copy-start.3 = (bf16[256,2048]{1,0:T(8,128)(2,1)S(1)}, bf16[256,2048]{1,0:T(8,128)(2,1)}, u32[]{:S(2)}) copy-start(bf16[256,2048]{1,0:T(8,128)(2,1)} %get-tuple-element.31) | copy-start | bytes 3145732
  245.8 5.9 %copy-start.2 = (bf16[256,2048]{1,0:T(8,128)(2,1)S(1)}, bf16[256,2048]{1,0:T(8,128)(2,1)}, u32[]{:S(2)}) copy-start(bf16[256,2048]{1,0:T(8,128)(2,1)} %get-tuple-element.32) | copy-start | bytes 3145732

commit v2 on v1

--- a/solution.py
+++ b/solution.py
@@ -788,6 +788,7 @@
 
 
 SPLIT = 4
+PACKED = 768
 STEP = 256
 
 
@@ -938,19 +939,65 @@
     sums = RowSums(team, m.sum_mine, m.sum_came, m.sum_send, m.sum_recv)
     deal = Deal(count, shard, width)
 
+    class Return:
+        def __init__(self, lot, source, target):
+            self.lot, self.source = lot, source
+            self.room = (m.parked, m.parked_too)[lot]
+            start = wires.book(2 * count)
+            self.parked = [
+                wires.copy(
+                    source.at[deal.at(peer(step))],
+                    self.room.at[me],
+                    (peer(step), team.me),
+                    start + step,
+                )
+                for step in range(1, count)
+            ]
+            goal = target.at[deal.at(me, team.slot * shard)]
+            self.placed = [
+                wires.copy(
+                    m.back_leaving.at[peer(step), lot],
+                    goal,
+                    (peer(step), team.me),
+                    start + count + step,
+                )
+                for step in range(1, count)
+            ]
+            self.placed.append(
+                pltpu.make_async_copy(m.back_leaving.at[me, lot], goal, m.put.at[lot])
+            )
+            self.holders = [holder(peer(step)) for step in range(count)]
+
+        def park(self):
+            for copy in self.parked:
+                copy.start()
+            self.room[me] = self.source[deal.at(me)]
+
+        def place(self):
+            for copy in self.parked:
+                copy.wait()
+            for step in range(count):
+                m.back_leaving[peer(step), self.lot] = self.room[self.holders[step]]
+            for copy in self.placed:
+                copy.start()
+
+        def wait(self):
+            for copy in self.placed:
+                copy.wait()
+
     loads["grad"].wait()
     dealt = wires.book(2 * count)
     first = []
     for step in range(1, count):
         copy = wires.copy(
             m.closed.at[deal.at(peer(step))],
-            m.back_parked.at[me, 0],
+            m.parked.at[me],
             (peer(step), team.me),
             dealt + step,
         )
         copy.start()
         first.append(copy)
-    m.back_parked[me, 0] = m.closed[deal.at(me)]
+    m.parked[me] = m.closed[deal.at(me)]
 
     loads["hid"].wait()
 
@@ -984,8 +1031,8 @@
     for copy in first:
         copy.wait()
     for step in range(1, count):
-        m.back_leaving[peer(step), 0] = m.back_parked[m.order[peer(step)], 0]
-    m.grad_in[deal.at(me)] = m.back_parked[m.order[me], 0]
+        m.back_leaving[peer(step), 0] = m.parked[m.order[peer(step)]]
+    m.grad_in[deal.at(me)] = m.parked[m.order[me]]
     second = []
     for step in range(1, count):
         copy = wires.copy(
@@ -1079,6 +1126,8 @@
     dm_gather.start()
     dm_spread = Spread(wires, grid, team, own_back, m.dm_all)
     dm_spread.start()
+    layer_return = Return(1, m.layer, m.layer_out)
+    layer_return.park()
     dm_gather.half()
     m.stats[0:1, :] = jnp.sum(m.fold[0], axis=0, keepdims=True)
     for i in range(3):
@@ -1103,7 +1152,9 @@
             right_inner(m.gate[...], m.wg[at, :]) + right_inner(m.upper[...], m.wu[at, :])
         ).astype(BF16)
 
-    reduce.run(make_d_mid)
+    reduce.begin(make_d_mid)
+    dm_spread.side(1)
+    reduce.end()
     m.fold[0] = jnp.zeros_like(m.fold[0])
 
     def norm_d_mid(at):
@@ -1121,6 +1172,7 @@
     over_rows(shard, 16, norm_d_mid)
     d_gather = gather(m.d_branch, 2)
     d_gather.start()
+    dm_spread.side(1)
     m.stats[1:2, :] = jnp.sum(m.fold[0], axis=0, keepdims=True)
     d_gather.half()
     d_gather.finish()
@@ -1179,6 +1231,8 @@
     for copy in stat_team:
         copy.start()
 
+    layer_return.place()
+
     def make_input(at):
         m.partial[:, at] = (
             right_inner(m.d_heads[:, 0:local], m.qkv[0, at, :])
@@ -1249,37 +1303,10 @@
 
     tiles = hidden // STEP
     stat_dp = [
-        wires.copy(m.stats, m.stat_dp.at[me], (peer(step), team.me), stat_at + 2 + step)
+        wires.copy(m.pack, m.stat_dp.at[me], (peer(step), team.me), stat_at + 2 + step)
         for step in range(1, count)
     ]
-    returned = wires.book(4 * count)
-    parked = [
-        wires.copy(
-            source.at[deal.at(peer(step))],
-            m.back_parked.at[me, i],
-            (peer(step), team.me),
-            returned + i * count + step,
-        )
-        for step in range(1, count)
-        for i, source in enumerate((m.layer, m.closed))
-    ]
-    placed = [
-        wires.copy(
-            m.back_leaving.at[peer(step), i],
-            target.at[deal.at(me, team.slot * shard)],
-            (peer(step), team.me),
-            returned + (2 + i) * count + step,
-        )
-        if step
-        else pltpu.make_async_copy(
-            m.back_leaving.at[me, i],
-            target.at[deal.at(me, team.slot * shard)],
-            m.put.at[i],
-        )
-        for step in range(count)
-        for i, target in enumerate((m.layer_out, m.input_grad))
-    ]
-    holders = [holder(peer(step)) for step in range(count)]
+    grad_return = Return(0, m.closed, m.input_grad)
     out_gathers = [gather(m.layer_out, 3), gather(m.input_grad, 4)]
 
     def add_stats():
@@ -1287,8 +1314,21 @@
             copy.wait()
         total = (m.stat_team[0] + m.stat_team[1]) + (m.stat_team[2] + m.stat_team[3])
         line = lax.broadcasted_iota(jnp.int32, total.shape, 0)
-        m.stats[...] = jnp.where(line == 2, m.stats[...], total)
-        m.stat_dp[me] = m.stats[...]
+        total = jnp.where(line == 2, m.stats[...], total)
+        m.pack[...] = jnp.zeros_like(m.pack)
+        packed = m.pack.shape[1]
+        for i in range(2):
+            for j in range(pl.cdiv(width, packed)):
+                piece = total[i : i + 1, j * packed : min((j + 1) * packed, width)]
+                m.pack[3 * i + j : 3 * i + j + 1, 0 : piece.shape[1]] = piece
+        m.pack[6:7, :] = total[2:3, 0:packed]
+        m.pack[7:8, 0 : 2 * local - packed] = total[2:3, packed : 2 * local]
+        for i in range(3):
+            square = jnp.sum(total[3 + i : 4 + i, :], axis=1, keepdims=True)
+            m.pack[7:8, 2 * local - packed + i * 128 : 2 * local - packed + (i + 1) * 128] = (
+                jnp.broadcast_to(square, (1, 128))
+            )
+        m.stat_dp[me] = m.pack[...]
         for copy in stat_dp:
             copy.start()
 
@@ -1299,24 +1339,12 @@
     def park():
         reduce.end()
         over_rows(shard, 16, close)
-        for copy in parked:
-            copy.start()
-        for i, source in enumerate((m.layer, m.closed)):
-            m.back_parked[me, i] = source[deal.at(me)]
+        grad_return.park()
         hid_spread.side(groups)
 
-    def place():
-        for copy in parked:
-            copy.wait()
-        for step in range(count):
-            for i in range(2):
-                m.back_leaving[peer(step), i] = m.back_parked[holders[step], i]
-        for copy in placed:
-            copy.start()
-
     def share():
-        for copy in placed:
-            copy.wait()
+        layer_return.wait()
+        grad_return.wait()
         for one in out_gathers:
             one.start()
 
@@ -1433,7 +1461,7 @@
     lax.fori_loop(1, groups, project_again, 0)
     wide_sums.start(m.wide_inner[:, 0:1], m.wide_inner[:, 1:2])
     branch_spread.pair(groups)
-    place()
+    grad_return.place()
     branch_spread.drain()
     for k in range(1, groups):
         bring(m.branch_all.at[k], m.dm_all.at[k])
@@ -1606,7 +1634,7 @@
         ("x_o", (local, tile), BF16),
         ("hid_all", (groups, rows, width), BF16),
         ("branch_all", (groups, rows, width), BF16),
-        ("stat_out", (8, width), F32),
+        ("stat_out", (8, PACKED), F32),
     ]
     wires = 160
     scratch = [
@@ -1638,12 +1666,14 @@
         ("layer", pltpu.VMEM((shard, width), BF16)),
         ("closed", pltpu.VMEM((shard, width), BF16)),
         ("grad_in", pltpu.VMEM((shard, width), BF16)),
-        ("back_parked", pltpu.VMEM((count, 2) + chunk, BF16)),
+        ("parked", pltpu.VMEM((count,) + chunk, BF16)),
+        ("parked_too", pltpu.VMEM((count,) + chunk, BF16)),
         ("back_leaving", pltpu.VMEM((count, 2) + chunk, BF16)),
         ("fold", pltpu.VMEM((4, 8, width), F32)),
         ("stats", pltpu.VMEM((8, width), F32)),
         ("stat_team", pltpu.VMEM((SLOTS, 8, width), F32)),
-        ("stat_dp", pltpu.VMEM((count, 8, width), F32)),
+        ("pack", pltpu.VMEM((8, PACKED), F32)),
+        ("stat_dp", pltpu.VMEM((count, 8, PACKED), F32)),
         ("partial", pltpu.VMEM((rows, width), BF16)),
         ("came", pltpu.VMEM((3, shard, width), BF16)),
         ("gone", pltpu.VMEM((shard, width), BF16)),
@@ -1712,7 +1742,7 @@
     rows = hidden_in.shape[1]
     width = hidden_in.shape[2]
     shard = rows // ways
-    if grid.lanes == 2 and grid.groups * rows + width // count <= width:
+    if grid.lanes == 2 and 2 * query_weight.shape[1] + 3 * 128 <= 2 * PACKED and width <= 3 * PACKED and grid.groups * rows + width // count <= width:
         cosine, sine = rope_constants(rows, HEAD)
         found = whole_layer(
             grid,
@@ -1742,7 +1772,8 @@
             return found[own] + found[other].astype(F32)
 
         stats = found["stat_out"]
-        squares = jnp.sum(stats[3:6], axis=1)
+        gains = stats[6:8].reshape(-1)
+        squares = gains[2 * local : 2 * local + 3 * 128 : 128]
         return (
             found["layer_out"][None],
             found["input_grad"][None],
@@ -1750,13 +1781,13 @@
             joined("k_own", "x_k"),
             joined("v_own", "x_v"),
             joined("o_own", "x_o"),
-            stats[2, :local],
-            stats[2, local : 2 * local],
-            stats[1],
+            gains[:local],
+            gains[local : 2 * local],
+            stats[3:6].reshape(-1)[:width],
             joined("g_own", "x_gate"),
             joined("u_own", "x_up"),
             joined("d_own", "x_down"),
-            stats[0],
+            stats[0:3].reshape(-1)[:width],
             jnp.sqrt(squares / (jnp.sum(seq_lengths).astype(F32) * D)),
         )
 

time: 253 us -> 239 us (0.945)
  Pallas kernels: 236 us -> 221 us
    pallas_call x1, Pallas kernels: 236 us -> 221 us  [whole_layer(): pl.pallas_call(functools.partial(layer_kernel, names), out_shape=shaped(*...]
where the time goes in v2:
time: 239 us
  Pallas kernels  221 us (92%)
  other arithmetic  11.4 us (5%)
  local copies, waits for them, and re-layouts  4.72 us (2%)
    pallas_call x1, Pallas kernels, whole_layer(): pl.pallas_call(functools.partial(layer_kernel, names), out_shape=shaped(*...  221 us
    add x5, other arithmetic, joined(): return found[own] + found[other].astype(F32)  10.3 us

profile of v2, /device:TPU:0, one launch (start us, length us, event | category | flops | bytes accessed | tf_op | source)
XLA Modules:
  0.0 238.9 jit_solution(11826426929553938957)
XLA Ops:
  0.7 221.3 %whole_layer.1 = (bf16[256,2048]{1,0:T(8,128)(2,1)}, bf16[256,2048]{1,0:T(8,128)(2,1)}, f32[256,2048]{1,0:T(8,128)}, f32[256,2048]{1,0:T(8,128)}, f32[2048,256]{...) custom-call(s32[8]{0:T(128)} %refs_0_.1, ...), custom_call_target="tpu_custom_call" | custom-call | tf_op jit(solution)/shard_map/whole_layer/pallas_call | solution.py:1702
  222.0 0.0 copy-start.4
  222.0 0.0 copy-start.5
  222.0 0.0 copy-start.10
  222.0 0.0 copy-start.11
  222.0 0.0 copy-start.1
  222.1 5.8 %convert_add_fusion.1 = (f32[256,2048]{1,0:T(8,128)}, f32[256,2048]{1,0:T(8,128)}) fusion(f32[256,2048]{1,0:T(8,128)} %get-tuple-element.44, bf16[256,2048]{1,0:T(8,128)(2,1)} %get-tuple-element.45, f32[256,2048]{1,0:T(8,128)} %get-tuple-element.42, bf16[256,2048]{1,0:T(8,128)(2,1)} %get-tuple-element.43), kind=kLoop, calls=%fused_computation.1 | loop fusion | flops 2097152 | bytes 10485760 | tf_op jit(solution)/shard_map/add | solution.py:1772
  227.9 0.0 copy-done.4
  227.9 0.0 copy-done.5
  227.9 0.0 copy-done.10
  227.9 0.0 copy-done.11
  227.9 1.1 convert_add_fusion.4
  229.1 0.0 copy-done.1
  229.1 0.8 copy-done
  229.9 1.6 convert_add_fusion
  231.5 0.0 copy-done.7
  231.5 0.0 copy-done.9
  231.5 0.8 convert_add_fusion.3
  232.3 0.0 copy-done.6
  232.4 0.0 copy-done.8
  232.4 0.9 convert_add_fusion.6
  233.2 0.0 copy-done.12
  233.2 0.6 fusion.1
  233.9 0.6 slice.34
  234.5 0.6 slice.35
  235.1 0.1 slice.31
  235.2 0.0 copy-done.13
  235.2 0.6 reduce_sum.9
  236.4 0.5 divide_sqrt_fusion
  237.0 0.0 copy-done.3
  237.0 1.0 copy.33
  237.9 1.0 copy.34
  (15 shorter events, 0.1 us)
Async XLA Ops:
  222.0 5.9 %copy-start.4 = (f32[256,512]{1,0:T(8,128)S(1)}, f32[256,512]{1,0:T(8,128)}, u32[]{:S(2)}) copy-start(f32[256,512]{1,0:T(8,128)} %get-tuple-element.35) | copy-start | bytes 1572868
  222.0 5.9 %copy-start.5 = (f32[256,512]{1,0:T(8,128)S(1)}, f32[256,512]{1,0:T(8,128)}, u32[]{:S(2)}) copy-start(f32[256,512]{1,0:T(8,128)} %get-tuple-element.37) | copy-start | bytes 1572868
  222.0 5.9 %copy-start.10 = (bf16[256,512]{1,0:T(8,128)(2,1)S(1)}, bf16[256,512]{1,0:T(8,128)(2,1)}, u32[]{:S(2)}) copy-start(bf16[256,512]{1,0:T(8,128)(2,1)} %get-tuple-element.36) | copy-start | bytes 786436
  222.0 5.9 %copy-start.11 = (bf16[256,512]{1,0:T(8,128)(2,1)S(1)}, bf16[256,512]{1,0:T(8,128)(2,1)}, u32[]{:S(2)}) copy-start(bf16[256,512]{1,0:T(8,128)(2,1)} %get-tuple-element.38) | copy-start | bytes 786436
  222.0 7.0 %copy-start.1 = (bf16[2048,256]{1,0:T(8,128)(2,1)S(1)}, bf16[2048,256]{1,0:T(8,128)(2,1)}, u32[]{:S(2)}) copy-start(bf16[2048,256]{1,0:T(8,128)(2,1)} %get-tuple-element.47) | copy-start | bytes 3145732
  227.9 2.0 copy-start
  229.9 1.6 copy-start.7
  229.9 1.6 copy-start.9
  229.9 2.5 %copy-start.6 = (f32[256,512]{1,0:T(8,128)S(1)}, f32[256,512]{1,0:T(8,128)}, u32[]{:S(2)}) copy-start(f32[256,512]{1,0:T(8,128)} %get-tuple-element.33) | copy-start | bytes 1572868
  229.9 2.5 %copy-start.8 = (bf16[256,512]{1,0:T(8,128)(2,1)S(1)}, bf16[256,512]{1,0:T(8,128)(2,1)}, u32[]{:S(2)}) copy-start(bf16[256,512]{1,0:T(8,128)(2,1)} %get-tuple-element.34) | copy-start | bytes 786436
  231.5 1.7 copy-start.12
  231.5 3.7 %copy-start.13 = (s32[8]{0:T(128)S(1)}, s32[8]{0:T(128)}, u32[]{:S(2)}) copy-start(s32[8]{0:T(128)} %refs_0_.1) | copy-start | bytes 100
  231.5 5.5 %copy-start.3 = (bf16[256,2048]{1,0:T(8,128)(2,1)S(1)}, bf16[256,2048]{1,0:T(8,128)(2,1)}, u32[]{:S(2)}) copy-start(bf16[256,2048]{1,0:T(8,128)(2,1)} %get-tuple-element.31) | copy-start | bytes 3145732
  232.3 5.6 %copy-start.2 = (bf16[256,2048]{1,0:T(8,128)(2,1)S(1)}, bf16[256,2048]{1,0:T(8,128)(2,1)}, u32[]{:S(2)}) copy-start(bf16[256,2048]{1,0:T(8,128)(2,1)} %get-tuple-element.32) | copy-start | bytes 3145732

commit v3 on v2

--- a/solution.py
+++ b/solution.py
@@ -1240,8 +1240,6 @@
             + right_inner(m.d_heads[:, 2 * local : 3 * local], m.qkv[2, at, :])
         ).astype(BF16)
 
-    reduce.begin(make_input)
-
     mid_spread.drain()
     dm_spread.drain()
     for k in range(groups):
@@ -1297,6 +1295,10 @@
         m.wd[at, spare] = matmul(m.wd[at, 0:every], all_rows(m.dm_all, tile_of(1 - grid.lane))).astype(BF16)
         for copy in crossings(n):
             copy.start()
+        return carry
+
+    def again_with_events(n, carry):
+        again(n, carry)
         for place, event in events.items():
             pl.when(n == place)(event)
         return carry
@@ -1340,7 +1342,6 @@
         reduce.end()
         over_rows(shard, 16, close)
         grad_return.park()
-        hid_spread.side(groups)
 
     def share():
         layer_return.wait()
@@ -1349,12 +1350,15 @@
             one.start()
 
     events = {
-        0: add_stats,
-        1: park,
-        tiles - 3: lambda: hid_spread.pair(groups),
-        tiles - 2: lambda: branch_spread.side(groups),
+        2: park,
+        tiles - 4: lambda: hid_spread.pair(groups),
+        tiles - 3: lambda: branch_spread.side(groups),
     }
-    lax.fori_loop(0, tiles, again, 0)
+    lax.fori_loop(0, 1, again, 0)
+    reduce.begin(make_input)
+    hid_spread.side(groups)
+    add_stats()
+    lax.fori_loop(1, tiles, again_with_events, 0)
     hid_spread.drain()
     def put(source, target, index):
         return pltpu.make_async_copy(source, target, m.put.at[index])
@@ -1379,68 +1383,14 @@
 
     for k in range(1, groups):
         bring(m.hid_all.at[k], m.mid_all.at[k])
-    turned_own = m.mid_turned.at[at_rows(grid.lane * tile, tile)]
-    wide = m.stage.shape[2]
-    high = rows
-
-    def narrow_stage(slot):
-        return m.stage.at[slot, :, pl.ds(0, tile)]
-
-    def flush(copies, last, i, values):
-        @pl.when(i > 0)
-        def _():
-            for copy in copies(i - 1):
-                copy.wait()
-
-        for copy, slot, value in zip(copies(i), last, values, strict=True):
-            slot[...] = value
-            copy.start()
-
-    def wide_copies(i):
-        at = at_rows(i * wide, wide)
-        return [put(m.stage.at[0], m.g_own.at[:, at], 2), put(m.stage.at[1], m.u_own.at[:, at], 3)]
-
-    def wide_part(i, carry):
-        at = at_rows(i * wide, wide)
-        flush(
-            wide_copies,
-            (m.stage.at[0], m.stage.at[1]),
-            i,
-            [matmul(turned_own[...], weight[0:every, at]) for weight in (m.wg, m.wu)],
-        )
-        return carry
-
-    lax.fori_loop(0, hidden // wide, wide_part, 0)
-    for copy in wide_copies(hidden // wide - 1):
-        copy.wait()
-
-    def high_at(i, slot):
-        return at_rows((2 * i + slot) * high, high)
-
-    def high_copies(i):
-        return [put(narrow_stage(slot), m.d_own.at[high_at(i, slot), :], 2 + slot) for slot in range(2)]
-
-    def high_part(i, carry):
-        right = all_rows(m.dm_all, tile_of(grid.lane))
-        flush(
-            high_copies,
-            (narrow_stage(0), narrow_stage(1)),
-            i,
-            [matmul(m.wd[high_at(i, slot), 0:every], right) for slot in range(2)],
-        )
-        return carry
-
-    lax.fori_loop(0, hidden // high // 2, high_part, 0)
-    for copy in high_copies(hidden // high // 2 - 1):
-        copy.wait()
-
     for copy in late:
         copy.wait()
     for k in range(groups):
         source = m.mid_all.at[k] if k else m.hid
-        m.mid_turned[:, pl.ds(k * rows, rows)] = jnp.transpose(
-            source[:, at_rows(grid.group * strip, strip)]
-        )
+        for lane in range(lanes):
+            m.gate[:, pl.ds(lane * every + k * rows, rows)] = jnp.transpose(
+                source[:, at_rows(grid.group * strip + lane * tile, tile)]
+            )
     wide_sums = RowSums(
         team, m.wide_mine, m.wide_came.at[0], m.wide_send.at[0], m.wide_recv.at[0]
     )
@@ -1464,7 +1414,7 @@
     grad_return.place()
     branch_spread.drain()
     for k in range(1, groups):
-        bring(m.branch_all.at[k], m.dm_all.at[k])
+        bring(m.branch_all.at[k], m.mid_all.at[k])
     for copy in late[groups - 1 :]:
         copy.wait()
     q_total, k_total = wide_sums.finish()
@@ -1480,7 +1430,7 @@
         inside = at_rows((k - 1) * rows, rows)
         q_scale = m.wide_scales[inside, 0:1]
         k_scale = m.wide_scales[inside, 1:2]
-        d_mix[...] = right_inner(m.dm_all[k], m.wo[...]).astype(BF16)
+        d_mix[...] = right_inner(m.mid_all[k], m.wo[...]).astype(BF16)
         q_inner = jnp.zeros((rows, 1), F32)
         k_inner = jnp.zeros((rows, 1), F32)
 
@@ -1524,13 +1474,14 @@
     def o_part(lane):
         return left_inner(m.mix[...], m.d_branch[:, lane_of(lane)]) + left_inner(
             m.wu[others, 0:local],
-            m.dm_all[1:groups, :, lane_of(lane)].reshape(every - rows, tile),
+            m.mid_all[1:groups, :, lane_of(lane)].reshape(every - rows, tile),
         )
 
     def heads_part(lane, at):
-        turned = m.mid_turned.at[at_rows(lane * tile, tile)]
-        return matmul(turned[:, 0:rows], m.d_heads[:, at]) + matmul(
-            turned[:, rows:every], m.wg[others, at]
+        first = at_rows(lane * every, rows)
+        rest = pl.ds(pl.multiple_of(lane * every + rows, rows), every - rows)
+        return matmul(m.gate[:, first], m.d_heads[:, at]) + matmul(
+            m.gate[:, rest], m.wg[others, at]
         )
 
     last = wires.book(4)
@@ -1561,6 +1512,60 @@
         finals.append(wires.copy(spare, target, crossing, last + i))
         finals[-1].start()
     share()
+    turned_own = m.mid_turned.at[at_rows(grid.lane * tile, tile)]
+    wide = m.stage.shape[2]
+    high = rows
+
+    def narrow_stage(slot):
+        return m.stage.at[slot, :, pl.ds(0, tile)]
+
+    def flush(copies, last, i, values):
+        @pl.when(i > 0)
+        def _():
+            for copy in copies(i - 1):
+                copy.wait()
+
+        for copy, slot, value in zip(copies(i), last, values, strict=True):
+            slot[...] = value
+            copy.start()
+
+    def wide_copies(i):
+        at = at_rows(i * wide, wide)
+        return [put(m.stage.at[0], m.g_own.at[:, at], 2), put(m.stage.at[1], m.u_own.at[:, at], 3)]
+
+    def wide_part(i, carry):
+        at = at_rows(i * wide, wide)
+        flush(
+            wide_copies,
+            (m.stage.at[0], m.stage.at[1]),
+            i,
+            [matmul(turned_own[...], weight[0:every, at]) for weight in (m.wg, m.wu)],
+        )
+        return carry
+
+    lax.fori_loop(0, hidden // wide, wide_part, 0)
+    for copy in wide_copies(hidden // wide - 1):
+        copy.wait()
+
+    def high_at(i, slot):
+        return at_rows((2 * i + slot) * high, high)
+
+    def high_copies(i):
+        return [put(narrow_stage(slot), m.d_own.at[high_at(i, slot), :], 2 + slot) for slot in range(2)]
+
+    def high_part(i, carry):
+        right = all_rows(m.dm_all, tile_of(grid.lane))
+        flush(
+            high_copies,
+            (narrow_stage(0), narrow_stage(1)),
+            i,
+            [matmul(m.wd[high_at(i, slot), 0:every], right) for slot in range(2)],
+        )
+        return carry
+
+    lax.fori_loop(0, hidden // high // 2, high_part, 0)
+    for copy in high_copies(hidden // high // 2 - 1):
+        copy.wait()
     for i, target in enumerate((m.q_own, m.k_own, m.v_own)):
         store(heads_part(this, pl.ds(i * local, local)), target)
     output = o_part(this)
@@ -1742,7 +1747,7 @@
     rows = hidden_in.shape[1]
     width = hidden_in.shape[2]
     shard = rows // ways
-    if grid.lanes == 2 and 2 * query_weight.shape[1] + 3 * 128 <= 2 * PACKED and width <= 3 * PACKED and grid.groups * rows + width // count <= width:
+    if grid.lanes == 2 and 2 * query_weight.shape[1] + 3 * 128 <= 2 * PACKED and width <= 3 * PACKED and width // count == rows and grid.groups * rows + width // count <= width:
         cosine, sine = rope_constants(rows, HEAD)
         found = whole_layer(
             grid,

time: 239 us -> 236 us (0.987)
  Pallas kernels: 221 us -> 218 us
    pallas_call x1, Pallas kernels: 221 us -> 218 us  [whole_layer(): pl.pallas_call(functools.partial(layer_kernel, names), out_shape=shaped(*...]
where the time goes in v3:
time: 236 us
  Pallas kernels  218 us (92%)
  other arithmetic  11.4 us (5%)
  local copies, waits for them, and re-layouts  4.72 us (2%)
    pallas_call x1, Pallas kernels, whole_layer(): pl.pallas_call(functools.partial(layer_kernel, names), out_shape=shaped(*...  218 us
    add x5, other arithmetic, joined(): return found[own] + found[other].astype(F32)  10.3 us

profile of v3, /device:TPU:0, one launch (start us, length us, event | category | flops | bytes accessed | tf_op | source)
XLA Modules:
  0.0 235.9 jit_solution(2191699302076234664)
XLA Ops:
  0.7 218.4 %whole_layer.1 = (bf16[256,2048]{1,0:T(8,128)(2,1)}, bf16[256,2048]{1,0:T(8,128)(2,1)}, f32[256,2048]{1,0:T(8,128)}, f32[256,2048]{1,0:T(8,128)}, f32[2048,256]{...) custom-call(s32[8]{0:T(128)} %refs_0_.1, ...), custom_call_target="tpu_custom_call" | custom-call | tf_op jit(solution)/shard_map/whole_layer/pallas_call | solution.py:1707
  219.0 0.0 copy-start.4
  219.0 0.0 copy-start.5
  219.0 0.0 copy-start.10
  219.1 0.0 copy-start.11
  219.1 0.0 copy-start.1
  219.1 5.8 %convert_add_fusion.1 = (f32[256,2048]{1,0:T(8,128)}, f32[256,2048]{1,0:T(8,128)}) fusion(f32[256,2048]{1,0:T(8,128)} %get-tuple-element.44, bf16[256,2048]{1,0:T(8,128)(2,1)} %get-tuple-element.45, f32[256,2048]{1,0:T(8,128)} %get-tuple-element.42, bf16[256,2048]{1,0:T(8,128)(2,1)} %get-tuple-element.43), kind=kLoop, calls=%fused_computation.1 | loop fusion | flops 2097152 | bytes 10485760 | tf_op jit(solution)/shard_map/add | solution.py:1777
  224.9 0.0 copy-done.4
  224.9 0.0 copy-done.5
  224.9 0.0 copy-done.10
  224.9 0.0 copy-done.11
  225.0 1.1 convert_add_fusion.4
  226.1 0.0 copy-done.1
  226.1 0.8 copy-done
  226.9 1.6 convert_add_fusion
  228.5 0.0 copy-done.7
  228.5 0.0 copy-done.9
  228.5 0.8 convert_add_fusion.3
  229.4 0.0 copy-done.6
  229.4 0.0 copy-done.8
  229.4 0.9 convert_add_fusion.6
  230.2 0.0 copy-done.12
  230.3 0.6 fusion.1
  230.9 0.6 slice.34
  231.5 0.6 slice.35
  232.1 0.1 slice.31
  232.2 0.0 copy-done.13
  232.2 0.6 reduce_sum.9
  233.5 0.5 divide_sqrt_fusion
  234.0 0.0 copy-done.3
  234.0 1.0 copy.33
  235.0 1.0 copy.34
  (15 shorter events, 0.1 us)
Async XLA Ops:
  219.0 5.9 %copy-start.4 = (f32[256,512]{1,0:T(8,128)S(1)}, f32[256,512]{1,0:T(8,128)}, u32[]{:S(2)}) copy-start(f32[256,512]{1,0:T(8,128)} %get-tuple-element.35) | copy-start | bytes 1572868
  219.0 5.9 %copy-start.5 = (f32[256,512]{1,0:T(8,128)S(1)}, f32[256,512]{1,0:T(8,128)}, u32[]{:S(2)}) copy-start(f32[256,512]{1,0:T(8,128)} %get-tuple-element.37) | copy-start | bytes 1572868
  219.0 5.9 %copy-start.10 = (bf16[256,512]{1,0:T(8,128)(2,1)S(1)}, bf16[256,512]{1,0:T(8,128)(2,1)}, u32[]{:S(2)}) copy-start(bf16[256,512]{1,0:T(8,128)(2,1)} %get-tuple-element.36) | copy-start | bytes 786436
  219.1 5.9 %copy-start.11 = (bf16[256,512]{1,0:T(8,128)(2,1)S(1)}, bf16[256,512]{1,0:T(8,128)(2,1)}, u32[]{:S(2)}) copy-start(bf16[256,512]{1,0:T(8,128)(2,1)} %get-tuple-element.38) | copy-start | bytes 786436
  219.1 7.0 %copy-start.1 = (bf16[2048,256]{1,0:T(8,128)(2,1)S(1)}, bf16[2048,256]{1,0:T(8,128)(2,1)}, u32[]{:S(2)}) copy-start(bf16[2048,256]{1,0:T(8,128)(2,1)} %get-tuple-element.47) | copy-start | bytes 3145732
  224.9 2.0 copy-start
  226.9 1.6 copy-start.7
  226.9 1.6 copy-start.9
  226.9 2.5 %copy-start.6 = (f32[256,512]{1,0:T(8,128)S(1)}, f32[256,512]{1,0:T(8,128)}, u32[]{:S(2)}) copy-start(f32[256,512]{1,0:T(8,128)} %get-tuple-element.33) | copy-start | bytes 1572868
  226.9 2.5 %copy-start.8 = (bf16[256,512]{1,0:T(8,128)(2,1)S(1)}, bf16[256,512]{1,0:T(8,128)(2,1)}, u32[]{:S(2)}) copy-start(bf16[256,512]{1,0:T(8,128)(2,1)} %get-tuple-element.34) | copy-start | bytes 786436
  228.5 1.7 copy-start.12
  228.5 3.7 %copy-start.13 = (s32[8]{0:T(128)S(1)}, s32[8]{0:T(128)}, u32[]{:S(2)}) copy-start(s32[8]{0:T(128)} %refs_0_.1) | copy-start | bytes 100
  228.5 5.5 %copy-start.3 = (bf16[256,2048]{1,0:T(8,128)(2,1)S(1)}, bf16[256,2048]{1,0:T(8,128)(2,1)}, u32[]{:S(2)}) copy-start(bf16[256,2048]{1,0:T(8,128)(2,1)} %get-tuple-element.31) | copy-start | bytes 3145732
  229.4 5.6 %copy-start.2 = (bf16[256,2048]{1,0:T(8,128)(2,1)S(1)}, bf16[256,2048]{1,0:T(8,128)(2,1)}, u32[]{:S(2)}) copy-start(bf16[256,2048]{1,0:T(8,128)(2,1)} %get-tuple-element.32) | copy-start | bytes 3145732

commit v4 on v3

--- a/solution.py
+++ b/solution.py
@@ -1351,8 +1351,10 @@
 
     events = {
         2: park,
+        tiles - 5: lambda: hid_spread.pair(2),
         tiles - 4: lambda: hid_spread.pair(groups),
-        tiles - 3: lambda: branch_spread.side(groups),
+        tiles - 3: lambda: branch_spread.side(2),
+        tiles - 2: lambda: branch_spread.side(groups),
     }
     lax.fori_loop(0, 1, again, 0)
     reduce.begin(make_input)

time: 236 us -> 236 us (level)
  no operation moved by 1% of the time
where the time goes in v4:
time: 236 us
  Pallas kernels  218 us (92%)
  other arithmetic  11.4 us (5%)
  local copies, waits for them, and re-layouts  4.72 us (2%)
    pallas_call x1, Pallas kernels, whole_layer(): pl.pallas_call(functools.partial(layer_kernel, names), out_shape=shaped(*...  218 us
    add x5, other arithmetic, joined(): return found[own] + found[other].astype(F32)  10.3 us

profile of v4, /device:TPU:0, one launch (start us, length us, event | category | flops | bytes accessed | tf_op | source)
XLA Modules:
  0.0 235.9 jit_solution(1943533294020258961)
XLA Ops:
  0.7 218.4 %whole_layer.1 = (bf16[256,2048]{1,0:T(8,128)(2,1)}, bf16[256,2048]{1,0:T(8,128)(2,1)}, f32[256,2048]{1,0:T(8,128)}, f32[256,2048]{1,0:T(8,128)}, f32[2048,256]{...) custom-call(s32[8]{0:T(128)} %refs_0_.1, ...), custom_call_target="tpu_custom_call" | custom-call | tf_op jit(solution)/shard_map/whole_layer/pallas_call | solution.py:1709
  219.0 0.0 copy-start.4
  219.0 0.0 copy-start.5
  219.0 0.0 copy-start.10
  219.1 0.0 copy-start.11
  219.1 0.0 copy-start.1
  219.1 5.8 %convert_add_fusion.1 = (f32[256,2048]{1,0:T(8,128)}, f32[256,2048]{1,0:T(8,128)}) fusion(f32[256,2048]{1,0:T(8,128)} %get-tuple-element.44, bf16[256,2048]{1,0:T(8,128)(2,1)} %get-tuple-element.45, f32[256,2048]{1,0:T(8,128)} %get-tuple-element.42, bf16[256,2048]{1,0:T(8,128)(2,1)} %get-tuple-element.43), kind=kLoop, calls=%fused_computation.1 | loop fusion | flops 2097152 | bytes 10485760 | tf_op jit(solution)/shard_map/add | solution.py:1779
  224.9 0.0 copy-done.4
  224.9 0.0 copy-done.5
  224.9 0.0 copy-done.10
  224.9 0.0 copy-done.11
  225.0 1.1 convert_add_fusion.4
  226.1 0.0 copy-done.1
  226.1 0.8 copy-done
  226.9 1.6 convert_add_fusion
  228.5 0.0 copy-done.7
  228.5 0.0 copy-done.9
  228.5 0.8 convert_add_fusion.3
  229.4 0.0 copy-done.6
  229.4 0.0 copy-done.8
  229.4 0.9 convert_add_fusion.6
  230.2 0.0 copy-done.12
  230.3 0.6 fusion.1
  230.9 0.6 slice.34
  231.5 0.6 slice.35
  232.1 0.1 slice.31
  232.2 0.0 copy-done.13
  232.2 0.6 reduce_sum.9
  233.5 0.5 divide_sqrt_fusion
  234.0 0.0 copy-done.3
  234.0 1.0 copy.33
  235.0 1.0 copy.34
  (15 shorter events, 0.1 us)
Async XLA Ops:
  219.0 5.9 %copy-start.4 = (f32[256,512]{1,0:T(8,128)S(1)}, f32[256,512]{1,0:T(8,128)}, u32[]{:S(2)}) copy-start(f32[256,512]{1,0:T(8,128)} %get-tuple-element.35) | copy-start | bytes 1572868
  219.0 5.9 %copy-start.5 = (f32[256,512]{1,0:T(8,128)S(1)}, f32[256,512]{1,0:T(8,128)}, u32[]{:S(2)}) copy-start(f32[256,512]{1,0:T(8,128)} %get-tuple-element.37) | copy-start | bytes 1572868
  219.0 5.9 %copy-start.10 = (bf16[256,512]{1,0:T(8,128)(2,1)S(1)}, bf16[256,512]{1,0:T(8,128)(2,1)}, u32[]{:S(2)}) copy-start(bf16[256,512]{1,0:T(8,128)(2,1)} %get-tuple-element.36) | copy-start | bytes 786436
  219.1 5.9 %copy-start.11 = (bf16[256,512]{1,0:T(8,128)(2,1)S(1)}, bf16[256,512]{1,0:T(8,128)(2,1)}, u32[]{:S(2)}) copy-start(bf16[256,512]{1,0:T(8,128)(2,1)} %get-tuple-element.38) | copy-start | bytes 786436
  219.1 7.0 %copy-start.1 = (bf16[2048,256]{1,0:T(8,128)(2,1)S(1)}, bf16[2048,256]{1,0:T(8,128)(2,1)}, u32[]{:S(2)}) copy-start(bf16[2048,256]{1,0:T(8,128)(2,1)} %get-tuple-element.47) | copy-start | bytes 3145732
  224.9 2.0 copy-start
  226.9 1.6 copy-start.7
  226.9 1.6 copy-start.9
  226.9 2.5 %copy-start.6 = (f32[256,512]{1,0:T(8,128)S(1)}, f32[256,512]{1,0:T(8,128)}, u32[]{:S(2)}) copy-start(f32[256,512]{1,0:T(8,128)} %get-tuple-element.33) | copy-start | bytes 1572868
  226.9 2.5 %copy-start.8 = (bf16[256,512]{1,0:T(8,128)(2,1)S(1)}, bf16[256,512]{1,0:T(8,128)(2,1)}, u32[]{:S(2)}) copy-start(bf16[256,512]{1,0:T(8,128)(2,1)} %get-tuple-element.34) | copy-start | bytes 786436
  228.5 1.7 copy-start.12
  228.5 3.7 %copy-start.13 = (s32[8]{0:T(128)S(1)}, s32[8]{0:T(128)}, u32[]{:S(2)}) copy-start(s32[8]{0:T(128)} %refs_0_.1) | copy-start | bytes 100
  228.5 5.5 %copy-start.3 = (bf16[256,2048]{1,0:T(8,128)(2,1)S(1)}, bf16[256,2048]{1,0:T(8,128)(2,1)}, u32[]{:S(2)}) copy-start(bf16[256,2048]{1,0:T(8,128)(2,1)} %get-tuple-element.31) | copy-start | bytes 3145732
  229.4 5.6 %copy-start.2 = (bf16[256,2048]{1,0:T(8,128)(2,1)S(1)}, bf16[256,2048]{1,0:T(8,128)(2,1)}, u32[]{:S(2)}) copy-start(bf16[256,2048]{1,0:T(8,128)(2,1)} %get-tuple-element.32) | copy-start | bytes 3145732
